TPU v7x, 32 devices: a whole 2x2x4 slice. The times are simulated.
32 devices in a mesh: gx: 4 (over y, core), gy: 8 (over z, x).
Axes of the slice: x: 2, y: 2, z: 4, core: 2. Of those that a mesh axis runs over, the one named last changes fastest.
Arguments:
- tokens: bfloat16 [256, 4096], P('gy', 'gx'), may hold values from -140 to 140
- cotangent: bfloat16 [256, 4096], P('gy', 'gx'), may hold values from -6 to 6
- gate_weight: bfloat16 [4096, 14336], P('gx', 'gy'), may hold values from -5 to 5
- up_weight: bfloat16 [4096, 14336], P('gx', 'gy'), may hold values from -5 to 5
- down_weight: bfloat16 [14336, 4096], P('gy', 'gx'), may hold values from -5 to 5
Outputs:
- output: bfloat16 [256, 4096], P('gy', 'gx')
- input_grad: bfloat16 [256, 4096], P('gy', 'gx')
- gate_grad: bfloat16 [4096, 14336], P('gx', 'gy')
- up_grad: bfloat16 [4096, 14336], P('gx', 'gy')
- down_grad: bfloat16 [14336, 4096], P('gy', 'gx')
All inputs are finite; a program needn't handle non-finite values.
Results may differ from a plain program's by a relative error of at most 0.005.
The roundings to bfloat16 on the way count: a program that leaves them out, or rounds other values in their place, can miss the bound.
Values may be sent and summed in bfloat16 or wider, within the bound.
A program may use at most 128 MiB of HBM per device.

v0:
```python
import functools

import jax
import jax.numpy as jnp
from jax import lax
from jax.experimental import pallas as pl
from jax.experimental.pallas import tpu as pltpu
from jax.sharding import PartitionSpec as P

ROT_BLOCK = 128
HID_BLOCK = 64
CORES = 2

fp_top = 448.0
tiny = 1e-06

MESH = pl.DeviceIdType.MESH
VMEM = pl.BlockSpec(memory_space=pltpu.VMEM)
DMA = pltpu.SemaphoreType.DMA


def hadamard_table(block_size):
    row_ids = jnp.arange(block_size, dtype=jnp.int32)[:, None]
    col_ids = jnp.arange(block_size, dtype=jnp.int32)[None, :]
    shared = row_ids & col_ids
    parity = jnp.zeros((block_size, block_size), jnp.int32)
    for bit_pos in range(max(block_size.bit_length() - 1, 1)):
        parity = parity + (shared >> bit_pos & 1)
    return (1 - 2 * (parity % 2)).astype(jnp.float32)


def rotate_cols(matrix, block_size):
    row_total, col_total = matrix.shape
    table = hadamard_table(block_size)
    blocks = matrix.reshape(row_total, col_total // block_size, block_size)
    if matrix.dtype == jnp.bfloat16:
        turned = jnp.einsum(
            "rbk,kl->rbl", blocks, table.astype(jnp.bfloat16), preferred_element_type=jnp.float32
        )
    else:
        turned = jnp.einsum("rbk,kl->rbl", blocks, table, precision=lax.Precision.HIGHEST)
    return turned.reshape(row_total, col_total) * block_size ** (-0.5)


def rotate_rows(matrix, block_size):
    row_total, col_total = matrix.shape
    table = hadamard_table(block_size)
    blocks = matrix.reshape(row_total // block_size, block_size, col_total)
    turned = jnp.einsum(
        "kl,bkc->blc", table.astype(jnp.bfloat16), blocks, preferred_element_type=jnp.float32
    )
    return turned.reshape(row_total, col_total) * block_size ** (-0.5)


def soft_cast(values, top):
    return (fp_top * jnp.tanh(values / top)).astype(jnp.bfloat16)


def peak(values):
    return jnp.max(jnp.abs(values))


def contract_rows(left_mat, right_mat):
    return lax.dot_general(
        left_mat, right_mat, (((0,), (0,)), ((), ())), preferred_element_type=jnp.float32
    )


def contract_cols(left_mat, right_mat):
    return lax.dot_general(
        left_mat, right_mat, (((1,), (1,)), ((), ())), preferred_element_type=jnp.float32
    )


def remote(src, dst, send, recv, target):
    return pltpu.make_async_remote_copy(
        src_ref=src, dst_ref=dst, send_sem=send, recv_sem=recv,
        device_id=target, device_id_type=MESH,
    )


def loop(low, high, body):
    def step(i, carry):
        body(i)
        return carry
    lax.fori_loop(low, high, step, 0)


def greet(n, me, axis):
    barrier = pltpu.get_barrier_semaphore()

    def hello(k):
        pl.semaphore_signal(
            barrier, inc=1, device_id={axis: lax.rem(me + k, n)}, device_id_type=MESH
        )

    loop(1, n, hello)


def exchange(n, me, axis, src, slots, send, recv):
    def copy(k, slot):
        return remote(
            src, slots.at[slot], send.at[k], recv.at[k], {axis: lax.rem(me + k, n)}
        )

    def start(k):
        copy(k, me).start()

    def finish(k):
        copy(k, lax.rem(me + n - k, n)).wait()

    return (lambda: loop(1, n, start)), (lambda: loop(1, n, finish))


def scatter_kernel(axis, n, inner, count, *refs):
    parts, outs = refs[:count], refs[count : 2 * count]
    first = refs[2 * count : 3 * count]
    second = refs[3 * count : 4 * count]
    third = refs[4 * count : 5 * count]
    s1, r1, s2, r2 = refs[5 * count :]
    me = lax.axis_index(axis)
    hi, lo = me // inner, lax.rem(me, inner)
    outer = n // inner
    greet(n, me, axis)
    pl.semaphore_wait(pltpu.get_barrier_semaphore(), n - 1)
    rows = outs[0].shape[0]
    step = 16

    def near(i, k, o):
        j, to = lax.rem(hi + k, outer), lax.rem(lo + o, inner)
        return remote(
            parts[i].at[inner * j + to], first[i].at[k * inner + o], s1.at[i, k, o],
            r1.at[i, k, o], {axis: inner * hi + to},
        )

    def far(i, k):
        j = lax.rem(hi + k, outer)
        return remote(
            second[i].at[k], third[i].at[k], s2.at[i, k], r2.at[i, k], {axis: inner * j + lo}
        )

    def inner_sum(i, k, at):
        total = parts[i][inner * lax.rem(hi + k, outer) + lo, at, :].astype(jnp.float32)
        for o in range(1, inner):
            total = total + first[i][k * inner + o, at, :].astype(jnp.float32)
        return total

    order = list(range(1, outer)) + [0]
    for k in order:
        for i in range(count):
            for o in range(1, inner):
                near(i, k, o).start()
    for k in order[:-1]:
        for i in range(count):
            for o in range(1, inner):
                near(i, k, o).wait()

            def add(r, i=i, k=k):
                at = pl.ds(pl.multiple_of(r * step, step), step)
                second[i][k, at, :] = inner_sum(i, k, at).astype(jnp.bfloat16)

            loop(0, rows // step, add)
            far(i, k).start()
    for i in range(count):
        for o in range(1, inner):
            near(i, 0, o).wait()
    for i in range(count):
        for k in order[:-1]:
            far(i, k).wait()

        def close(r, i=i):
            at = pl.ds(pl.multiple_of(r * step, step), step)
            total = inner_sum(i, 0, at)
            for k in order[:-1]:
                total = total + third[i][k, at, :].astype(jnp.float32)
            outs[i][at, :] = total

        loop(0, rows // step, close)


def scatter(axis, n, inner, parts, number):
    count, outer = len(parts), n // inner
    near = [pltpu.VMEM((n,) + p.shape[1:], p.dtype) for p in parts]
    far = [pltpu.VMEM((outer,) + p.shape[1:], jnp.bfloat16) for p in parts]
    return pl.pallas_call(
        functools.partial(scatter_kernel, axis, n, inner, count),
        out_shape=[jax.ShapeDtypeStruct(p.shape[1:], jnp.float32) for p in parts],
        in_specs=[VMEM] * count,
        out_specs=[VMEM] * count,
        scratch_shapes=near + far * 2
        + [DMA((count, outer, inner))] * 2 + [DMA((count, outer))] * 2,
        compiler_params=pltpu.CompilerParams(collective_id=number, has_side_effects=True),
    )(*parts)


def gather_kernel(axis, n, inner, nx, ny, count, *refs):
    blocks, tile = refs[:count], refs[count]
    outs, tile_out = refs[count + 1 : 2 * count + 1], refs[2 * count + 1]
    slots_x, slots_y, mid, sn, rn, sf, rf, sx, rx, sy, ry = refs[2 * count + 2 :]
    gx, gy = lax.axis_index("gx"), lax.axis_index("gy")
    me = lax.axis_index(axis)
    hi, lo = me // inner, lax.rem(me, inner)
    outer = n // inner
    greet(nx, gx, "gx")
    greet(ny, gy, "gy")
    pl.semaphore_wait(pltpu.get_barrier_semaphore(), nx - 1 + ny - 1)

    start_x, finish_x = exchange(nx, gx, "gx", tile, slots_x, sx, rx)
    start_y, finish_y = exchange(ny, gy, "gy", mid, slots_y, sy, ry)
    start_x()

    def far(i, k, slot):
        j = lax.rem(hi + k, outer)
        return remote(
            blocks[i], outs[i].at[slot], sf.at[i, k], rf.at[i, k], {axis: inner * j + lo}
        )

    def near(i, k, o, src, slot):
        return remote(
            src, outs[i].at[slot], sn.at[i, k, o], rn.at[i, k, o],
            {axis: inner * hi + lax.rem(lo + o, inner)},
        )

    for k in range(1, outer):
        for i in range(count):
            far(i, k, me).start()
    for i in range(count):
        for o in range(1, inner):
            near(i, 0, o, blocks[i], me).start()
    slots_x[gx] = tile[...]
    for i in range(count):
        outs[i][me] = blocks[i][...]
    finish_x()
    mid[...] = jnp.max(slots_x[...], axis=0)
    start_y()
    slots_y[gy] = mid[...]
    for k in range(1, outer):
        mine = inner * lax.rem(hi + outer - k, outer) + lo
        for i in range(count):
            far(i, k, mine).wait()
            for o in range(1, inner):
                near(i, k, o, outs[i].at[mine], mine).start()
    finish_y()
    top = jnp.max(slots_y[...], axis=0)
    tile_out[0] = top
    tile_out[1] = top + tiny
    tile_out[2] = top / fp_top
    tile_out[3] = top * top[0:1, :] / (fp_top * fp_top)
    for i in range(count):
        for o in range(1, inner):
            side = lax.rem(lo + inner - o, inner)
            near(i, 0, o, blocks[i], inner * hi + side).wait()
            for k in range(1, outer):
                row = inner * lax.rem(hi + outer - k, outer)
                near(i, k, o, outs[i].at[row + lo], row + side).wait()


def gather(axis, n, inner, nx, ny, blocks, tile, number):
    count, outer = len(blocks), n // inner
    return pl.pallas_call(
        functools.partial(gather_kernel, axis, n, inner, nx, ny, count),
        out_shape=[jax.ShapeDtypeStruct((n,) + b.shape, b.dtype) for b in blocks]
        + [jax.ShapeDtypeStruct((4,) + tile.shape, tile.dtype)],
        in_specs=[VMEM] * (count + 1),
        out_specs=[VMEM] * (count + 1),
        scratch_shapes=[
            pltpu.VMEM((nx,) + tile.shape, tile.dtype),
            pltpu.VMEM((ny,) + tile.shape, tile.dtype),
            pltpu.VMEM(tile.shape, tile.dtype),
        ]
        + [DMA((count, outer, inner))] * 2 + [DMA((count, outer))] * 2
        + [DMA((nx,))] * 2 + [DMA((ny,))] * 2,
        compiler_params=pltpu.CompilerParams(collective_id=number, has_side_effects=True),
    )(*blocks, tile)


def peak_tile(values):
    rows = lax.broadcasted_iota(jnp.int32, (8, 128), 0)
    tile = jnp.full((8, 128), values[0])
    for i, value in enumerate(values[1:], 1):
        tile = jnp.where(rows == i, value, tile)
    return tile


def shards(nx, ny, tokens, cotangent, gate_weight, up_weight, down_weight):
    lanes = 1 << ((ny.bit_length() - 2) // 2)
    gate_rot = rotate_rows(gate_weight, ROT_BLOCK)
    up_rot = rotate_rows(up_weight, ROT_BLOCK)
    down_rot = rotate_rows(down_weight, HID_BLOCK)
    own_peaks = [
        peak(rotate_cols(tokens, ROT_BLOCK)), peak(gate_rot), peak(up_rot), peak(down_rot)
    ]
    all_tokens, all_cot, peaks = gather(
        "gy", ny, lanes, nx, ny, [tokens, cotangent], peak_tile(own_peaks), 0
    )
    down_peak = peaks[0, 3, 0]
    token_top, gate_top, up_top, down_top = (peaks[1, i, 0] for i in range(4))
    token_unit, gate_unit, up_unit, down_unit = (peaks[2, i, 0] for i in range(4))
    width = tokens.shape[1]
    all_tokens = all_tokens.reshape(-1, width)
    all_cot = all_cot.reshape(-1, width)
    token_total = all_tokens.shape[0]
    gate_cast = soft_cast(gate_rot, gate_top)
    up_cast = soft_cast(up_rot, up_top)
    down_cast = soft_cast(down_rot, down_top)
    hid_width = gate_weight.shape[1]
    token_cast = soft_cast(rotate_cols(all_tokens, ROT_BLOCK), token_top)

    def split(matrix, n):
        return matrix.reshape(n, token_total // n, matrix.shape[1])

    gate_sum, up_sum, back_sum = scatter(
        "gx", nx, CORES,
        [
            split(jnp.dot(token_cast, gate_cast, preferred_element_type=jnp.float32), nx),
            split(jnp.dot(token_cast, up_cast, preferred_element_type=jnp.float32), nx),
            split(contract_cols(all_cot, down_cast), nx),
        ],
        1,
    )
    gate_pre = gate_sum * peaks[3, 1, 0]
    up_pre = up_sum * peaks[3, 2, 0]
    sigmoid_gate = jax.nn.sigmoid(gate_pre)
    hidden = (gate_pre * sigmoid_gate * up_pre).astype(jnp.bfloat16)
    own_peak = peak(rotate_cols(hidden, HID_BLOCK))
    hidden_grad = rotate_cols(back_sum * down_unit, HID_BLOCK)
    gate_act = (
        hidden_grad * up_pre * sigmoid_gate * (1.0 + gate_pre * (1.0 - sigmoid_gate))
    ).astype(jnp.bfloat16)
    up_act = (hidden_grad * gate_pre * sigmoid_gate).astype(jnp.bfloat16)
    all_hidden, all_gate_act, all_up_act, tops = gather(
        "gx", nx, CORES, nx, ny, [hidden, gate_act, up_act], peak_tile([own_peak, down_peak]), 2
    )
    hidden_top, hidden_unit = tops[1, 0, 0], tops[2, 0, 0]
    all_hidden = all_hidden.reshape(-1, hid_width)
    all_gate_act = all_gate_act.reshape(-1, hid_width)
    all_up_act = all_up_act.reshape(-1, hid_width)
    hidden_cast = soft_cast(rotate_cols(all_hidden, HID_BLOCK), hidden_top)
    out_part = jnp.dot(hidden_cast, down_cast, preferred_element_type=jnp.float32)
    input_part = contract_cols(all_gate_act, gate_cast) * gate_unit + contract_cols(
        all_up_act, up_cast
    ) * up_unit
    out_sum, input_sum = scatter(
        "gy", ny, lanes,
        [split(part.astype(jnp.bfloat16), ny) for part in (out_part, input_part)],
        3,
    )
    output = (out_sum * tops[3, 1, 0]).astype(jnp.bfloat16)
    input_grad = rotate_cols(input_sum, ROT_BLOCK).astype(jnp.bfloat16)
    hidden_turned = rotate_cols(hidden_cast, HID_BLOCK).astype(jnp.bfloat16)
    token_turned = rotate_cols(token_cast, ROT_BLOCK).astype(jnp.bfloat16)
    down_grad = (contract_rows(hidden_turned, all_cot) * hidden_unit).astype(
        jnp.bfloat16
    )
    gate_grad = (contract_rows(token_turned, all_gate_act) * token_unit).astype(
        jnp.bfloat16
    )
    up_grad = (contract_rows(token_turned, all_up_act) * token_unit).astype(jnp.bfloat16)
    return (output, input_grad, gate_grad, up_grad, down_grad)


def solution(mesh):
    in_specs = (P("gy", "gx"), P("gy", "gx"), P("gx", "gy"), P("gx", "gy"), P("gy", "gx"))
    out_specs = (P("gy", "gx"), P("gy", "gx"), P("gx", "gy"), P("gx", "gy"), P("gy", "gx"))
    nx, ny = mesh.shape["gx"], mesh.shape["gy"]
    return jax.shard_map(
        functools.partial(shards, nx, ny),
        mesh=mesh, in_specs=in_specs, out_specs=out_specs, check_vma=False,
    )
```

profile of v0, /device:TPU:0, one launch (start us, length us, event | category | flops | bytes accessed | tf_op | source)
XLA Modules:
  0.0 186.8 jit_solution(14934206638692672424)
XLA Ops:
  0.6 1.7 fusion.24
  2.3 6.9 %abs_reduce_fusion = (f32[]{:T(128)}, f32[128,8,1792]{2,0,1:T(8,128)}) fusion(bf16[8,128,1792]{2,1,0:T(8,128)(2,1)} %bitcast.132), kind=kOutput, calls=%fused_computation.6 | convolution fusion | flops 475856896 | bytes 11010052 | tf_op jit(solution)/shard_map/kl,bkc->blc/dot_general | solution.py:49
  9.2 1.3 compare_select_fusion.1
  10.5 4.8 %abs_reduce_fusion.1 = (f32[]{:T(128)}, f32[128,8,1792]{2,0,1:T(8,128)}) fusion(bf16[8,128,1792]{2,1,0:T(8,128)(2,1)S(1)} %bitcast.133), kind=kOutput, calls=%fused_computation.7 | convolution fusion | flops 475856896 | bytes 11010052 | tf_op jit(solution)/shard_map/kl,bkc->blc/dot_general | solution.py:49
  15.3 4.7 %abs_reduce_fusion.2 = (f32[]{:T(128)}, f32[64,28,1024]{2,0,1:T(8,128)}) fusion(bf16[28,64,1024]{2,1,0:T(8,128)(2,1)S(1)} %bitcast.134), kind=kOutput, calls=%fused_computation.8 | convolution fusion | flops 240521216 | bytes 11010052 | tf_op jit(solution)/shard_map/kl,bkc->blc/dot_general | solution.py:49
  19.9 2.0 %select_select_fusion.refs_2_ = f32[8,128]{1,0:T(8,128)} fusion(f32[8]{0:T(128)S(1)} %compare_select_fusion.1, f32[]{:T(128)} %get-tuple-element.48, f32[]{:T(128)} %get-tuple-element.50, pred[8]{0:T(512)(128)(4,1)S(1)} %get-tuple-element.52, pred[8]{0:T(512)(128)(4,1)S(1)} %get-tuple-element.53), kind=kLoop, calls=%fused_computation.79 | loop fusion | flops 2048 | bytes 4152 | tf_op jit(solution)/shard_map/jit(_where)/select_n | solution.py:281
  21.9 24.4 %shard_map.92 = (bf16[8,32,1024]{2,1,0:T(8,128)(2,1)}, bf16[8,32,1024]{2,1,0:T(8,128)(2,1)}, f32[4,8,128]{2,1,0:T(8,128)}) custom-call(bf16[32,1024]{1,0:T(8,128)(2,1)} %refs_0_.1, bf16[32,1024]{1,0:T(8,128)(2,1)} %refs_1_.1, f32[8,128]{1,0:T(8,128)} %select_select_fusion.refs_2_), custom_call_target="tpu_custom_call" | custom-call | tf_op jit(solution)/shard_map/pallas_call | solution.py:260
  46.3 1.3 copy.49
  47.6 2.0 %fusion.137 = (f32[1,1,1]{2,1,0:T(1,128)}, f32[1,1,1]{2,1,0:T(1,128)}, f32[1,1,1]{2,1,0:T(1,128)}, f32[1,1,1]{2,1,0:T(1,128)}, f32[1,1,1]{2,1,0:T(1,128)}, /*ind...) fusion(f32[4,8,128]{2,1,0:T(8,128)} %get-tuple-element.18), kind=kLoop, calls=%fused_computation.157 | loop fusion | bytes 88 | tf_op jit(solution)/shard_map/slice | solution.py:298
  49.6 7.1 %multiply_convert_fusion.3 = bf16[64,28,1024]{2,0,1:T(8,128)(2,1)} fusion(f32[64,28,1024]{2,0,1:T(8,128)} %get-tuple-element.51, f32[]{:T(128)} %bitcast.17), kind=kLoop, calls=%fused_computation.3 | loop fusion | flops 7340032 | bytes 11010052 | tf_op jit(solution)/shard_map/convert
  56.7 3.5 %multiply_convert_fusion.4 = bf16[128,8,1792]{2,0,1:T(8,128)(2,1)} fusion(f32[128,8,1792]{2,0,1:T(8,128)S(1)} %bitcast.127, f32[]{:T(128)} %bitcast.12), kind=kLoop, calls=%fused_computation.4 | loop fusion | flops 7340032 | bytes 11010052 | tf_op jit(solution)/shard_map/convert.1
  60.2 3.7 %multiply_convert_fusion.5 = bf16[128,8,1792]{2,0,1:T(8,128)(2,1)} fusion(f32[128,8,1792]{2,0,1:T(8,128)S(1)} %bitcast.125, f32[]{:T(128)} %bitcast.8), kind=kLoop, calls=%fused_computation.5 | loop fusion | flops 7340032 | bytes 11010052 | tf_op jit(solution)/shard_map/convert.2
  63.9 1.1 fusion.16
  64.9 0.3 fusion.14
  65.3 0.3 copy.26
  65.7 0.2 convert_element_type.141
  65.9 0.2 copy.35
  66.1 4.5 %fusion.139.refs_1_ = f32[4,64,1792]{2,1,0:T(8,128)} fusion(bf16[4,64,1024]{2,1,0:T(8,128)(2,1)S(1)} %convert_element_type.141, bf16[1024,1792,1]{1,0,2:T(8,128)(2,1)} %bitcast.128), kind=kOutput, calls=%fused_computation.159 | convolution fusion | flops 939524096 | bytes 6029312 | tf_op jit(solution)/shard_map/dot_general | solution.py:316
  70.6 2.4 %fusion.138.refs_0_ = f32[4,64,1792]{2,1,0:T(8,128)} fusion(bf16[4,64,1024]{2,1,0:T(8,128)(2,1)S(1)} %convert_element_type.141, bf16[1024,1792,1]{1,0,2:T(8,128)(2,1)S(1)} %bitcast.130), kind=kOutput, calls=%fused_computation.158 | convolution fusion | flops 939524096 | bytes 6029312 | tf_op jit(solution)/shard_map/dot_general | solution.py:315
  73.0 2.5 %fusion.140.refs_2_ = f32[4,64,1792]{2,1,0:T(8,128)} fusion(bf16[4,64,1024]{2,1,0:T(8,128)(2,1)S(1)} %bitcast.151, bf16[1792,1024,1]{1,0,2:T(8,128)(2,1)S(1)} %bitcast.135), kind=kOutput, calls=%fused_computation.160 | convolution fusion | flops 939524096 | bytes 6029312 | tf_op jit(solution)/shard_map/dot_general | solution.py:70
  75.5 23.7 %shard_map.93 = (f32[64,1792]{1,0:T(8,128)}, f32[64,1792]{1,0:T(8,128)}, f32[64,1792]{1,0:T(8,128)}) custom-call(f32[4,64,1792]{2,1,0:T(8,128)} %fusion.138.refs_0_, f32[4,64,1792]{2,1,0:T(8,128)} %fusion.139.refs_1_, f32[4,64,1792]{2,1,0:T(8,128)} %fusion.140.refs_2_), custom_call_target="tpu_custom_call" | custom-call | tf_op jit(solution)/shard_map/pallas_call | solution.py:185
  99.2 1.8 broadcast_multiply_fusion
  101.0 0.4 reshape.89
  101.4 1.5 convolution_multiply_fusion.4
  102.9 0.5 copy.29
  103.5 0.3 mul.246
  103.8 2.3 %multiply_convert_fusion.8 = (bf16[64,1792]{1,0:T(8,128)(2,1)}, bf16[64,1792]{1,0:T(8,128)(2,1)}, bf16[64,1792]{1,0:T(8,128)(2,1)S(1)}) fusion(f32[64,1792]{1,0:T(8,128)S(1)} %mul.246, f32[64,1792]{1,0:T(8,128)S(1)} %copy-done.8, f32[]{:T(128)} %bitcast.21, f32[64,1792]{1,0:T(8,128)S(1)} %copy-done.9, f32[]{:T(128)} %bitcast.22), kind=kLoop, calls=%fused_computation.40 | loop fusion | flops 2064384 | bytes 2064392 | tf_op jit(solution)/shard_map/convert_element_type | solution.py:330
  106.1 0.5 reshape.90
  106.6 1.1 fusion.23
  107.7 1.3 compare_select_fusion
  109.0 0.7 iota.60.refs_3_
  109.7 26.4 %shard_map.94 = (bf16[4,64,1792]{2,1,0:T(8,128)(2,1)}, bf16[4,64,1792]{2,1,0:T(8,128)(2,1)}, bf16[4,64,1792]{2,1,0:T(8,128)(2,1)}, f32[4,8,128]{2,1,0:T(8,128)}) custom-call(bf16[64,1792]{1,0:T(8,128)(2,1)} %copy-done.6, bf16[64,1792]{1,0:T(8,128)(2,1)} %get-tuple-element.30.refs_1_, bf16[64,1792]{1,0:T(8,128)(2,1)} %get-tuple-element.29.refs_2_, ...), custom_call_target="tpu_custom_call" | custom-call | tf_op jit(solution)/shard_map/pallas_call | solution.py:260
  136.1 4.7 %convolution_multiply_fusion = f32[256,1024]{1,0:T(8,128)S(1)} fusion(bf16[256,1792]{1,0:T(8,128)(2,1)} %bitcast.147, bf16[1024,1792]{1,0:T(8,128)(2,1)} %bitcast.129, f32[]{:T(128)} %bitcast.35), kind=kOutput, calls=%fused_computation.16 | convolution fusion | flops 939786240 | bytes 5636100 | tf_op jit(solution)/shard_map/dot_general | solution.py:70
  140.9 2.7 %fusion.15 = bf16[256,1024]{1,0:T(8,128)(2,1)} fusion(f32[256,1024]{1,0:T(8,128)S(1)} %convolution_multiply_fusion, bf16[256,1792]{1,0:T(8,128)(2,1)S(1)} %bitcast.149, bf16[1024,1792]{1,0:T(8,128)(2,1)S(1)} %bitcast.131, f32[]{:T(128)} %bitcast.32), kind=kOutput, calls=%fused_computation.28 | convolution fusion | flops 940310528 | bytes 6160388 | tf_op jit(solution)/shard_map/dot_general | solution.py:70
  143.5 1.2 fusion.136
  144.7 2.0 %reshape.108 = bf16[256,28,64]{2,1,0:T(8,128)(2,1)S(1)} reshape(bf16[4,64,1792]{2,1,0:T(8,128)(2,1)S(1)} %copy-done.7) | data formatting | bytes 1835008 | tf_op jit(solution)/shard_map/reshape;reshape | solution.py:35
  146.8 2.0 %multiply_convert_fusion.7 = bf16[256,28,64]{0,2,1:T(8,128)(2,1)S(1)} fusion(bf16[256,28,64]{2,1,0:T(8,128)(2,1)S(1)} %reshape.108, f32[]{:T(128)} %bitcast.27), kind=kOutput, calls=%fused_computation.14 | convolution fusion | flops 60690432 | bytes 1835012 | tf_op jit(solution)/shard_map/rbk,kl->rbl/dot_general | solution.py:37
  148.8 0.0 copy-done.5
  148.8 1.9 %fusion.17 = bf16[256,1024]{1,0:T(8,128)(2,1)} fusion(bf16[256,28,64]{0,2,1:T(8,128)(2,1)S(1)} %multiply_convert_fusion.7, bf16[64,28,1024]{2,0,1:T(8,128)(2,1)S(1)} %copy-done.5), kind=kOutput, calls=%fused_computation.30 | convolution fusion | flops 939786240 | bytes 5111808 | tf_op jit(solution)/shard_map/dot_general | solution.py:339
  150.7 0.4 multiply_convert_fusion.6
  151.2 20.7 %shard_map.95 = (f32[32,1024]{1,0:T(8,128)}, f32[32,1024]{1,0:T(8,128)}) custom-call(bf16[8,32,1024]{2,1,0:T(8,128)(2,1)} %bitcast.141, bf16[8,32,1024]{2,1,0:T(8,128)(2,1)} %bitcast.140), custom_call_target="tpu_custom_call" | custom-call | tf_op jit(solution)/shard_map/pallas_call | solution.py:185
  171.8 2.2 %multiply_convert_fusion.11 = bf16[32,1024]{1,0:T(8,128)(2,1)} fusion(f32[32,1024]{1,0:T(8,128)} %get-tuple-element.27, f32[]{:T(128)} %bitcast.37), kind=kLoop, calls=%fused_computation.45 | loop fusion | flops 65536 | bytes 196612 | tf_op jit(solution)/shard_map/convert_element_type | solution.py:348
  174.0 0.9 copy.50
  174.9 0.3 fusion.21
  175.3 0.6 copy.67
  175.9 3.6 %multiply_convert_fusion = bf16[1792,1024]{1,0:T(8,128)(2,1)} fusion(bf16[256,1792]{0,1:T(8,128)(2,1)S(1)} %bitcast.136, bf16[256,1024]{1,0:T(8,128)(2,1)S(1)} %bitcast.152, f32[]{:T(128)} %bitcast.43), kind=kOutput, calls=%fused_computation | convolution fusion | flops 943194112 | bytes 5111812 | tf_op jit(solution)/shard_map/dot_general | solution.py:64
  179.6 3.7 %multiply_convert_fusion.2 = bf16[1024,1792]{1,0:T(8,128)(2,1)} fusion(bf16[256,1024]{0,1:T(8,128)(2,1)S(1)} %bitcast.137, bf16[256,1792]{1,0:T(8,128)(2,1)S(1)} %bitcast.150, f32[]{:T(128)} %bitcast.40), kind=kOutput, calls=%fused_computation.2 | convolution fusion | flops 943194112 | bytes 5111812 | tf_op jit(solution)/shard_map/dot_general | solution.py:64
  183.2 3.6 %multiply_convert_fusion.1 = bf16[1024,1792]{1,0:T(8,128)(2,1)} fusion(bf16[256,1024]{0,1:T(8,128)(2,1)S(1)} %bitcast.138, bf16[256,1792]{1,0:T(8,128)(2,1)S(1)} %bitcast.148, f32[]{:T(128)} %bitcast.40), kind=kOutput, calls=%fused_computation.1 | convolution fusion | flops 943194112 | bytes 5111812 | tf_op jit(solution)/shard_map/dot_general | solution.py:64
  (40 shorter events, 0.1 us)
Async XLA Ops:
  2.3 8.2 %copy-start.2 = (bf16[1024,1792]{1,0:T(8,128)(2,1)S(1)}, bf16[1024,1792]{1,0:T(8,128)(2,1)}, u32[]{:S(2)}) copy-start(bf16[1024,1792]{1,0:T(8,128)(2,1)} %param.8) | copy-start | bytes 11010052
  10.5 4.8 %copy-start.3 = (bf16[1792,1024]{1,0:T(8,128)(2,1)S(1)}, bf16[1792,1024]{1,0:T(8,128)(2,1)}, u32[]{:S(2)}) copy-start(bf16[1792,1024]{1,0:T(8,128)(2,1)} %param.9) | copy-start | bytes 11010052
  15.3 41.4 %slice-start.2 = ((s8[7340032]{0:T(1024)(128)(4,1)}), s8[3145728]{0:T(1024)(128)(4,1)S(1)}, s32[]{:S(2)}) async-start(s8[7340032]{0:T(1024)(128)(4,1)} %bitcast.126), calls=%async_computation.2 | async-start | bytes 6291456
  46.3 10.4 %slice-start.3 = ((s8[7340032]{0:T(1024)(128)(4,1)}), s8[4194304]{0:T(1024)(128)(4,1)S(1)}, s32[]{:S(2)}) async-start(s8[7340032]{0:T(1024)(128)(4,1)} %bitcast.126), calls=%async_computation.3 | async-start | bytes 8388608
  46.3 13.9 %slice-start = ((s8[7340032]{0:T(1024)(128)(4,1)}), s8[4194304]{0:T(1024)(128)(4,1)S(1)}, s32[]{:S(2)}) async-start(s8[7340032]{0:T(1024)(128)(4,1)} %bitcast.124), calls=%async_computation | async-start | bytes 8388608
  49.6 10.6 %slice-start.1 = ((s8[7340032]{0:T(1024)(128)(4,1)}), s8[3145728]{0:T(1024)(128)(4,1)S(1)}, s32[]{:S(2)}) async-start(s8[7340032]{0:T(1024)(128)(4,1)} %bitcast.124), calls=%async_computation.1 | async-start | bytes 6291456
  66.1 4.5 %copy-start = (bf16[128,8,1792]{2,0,1:T(8,128)(2,1)S(1)}, bf16[128,8,1792]{2,0,1:T(8,128)(2,1)}, u32[]{:S(2)}) copy-start(bf16[128,8,1792]{2,0,1:T(8,128)(2,1)} %multiply_convert_fusion.5) | copy-start | bytes 11010052
  70.6 2.4 %copy-start.4 = (bf16[64,28,1024]{2,0,1:T(8,128)(2,1)S(1)}, bf16[64,28,1024]{2,0,1:T(8,128)(2,1)}, u32[]{:S(2)}) copy-start(bf16[64,28,1024]{2,0,1:T(8,128)(2,1)} %multiply_convert_fusion.3) | copy-start | bytes 11010052
  70.6 2.4 %copy-start.13 = (bf16[8,32,1024]{2,1,0:T(8,128)(2,1)S(1)}, bf16[8,32,1024]{2,1,0:T(8,128)(2,1)}, u32[]{:S(2)}) copy-start(bf16[8,32,1024]{2,1,0:T(8,128)(2,1)} %get-tuple-element.19) | copy-start | bytes 1572868
  99.2 4.6 %copy-start.8 = (f32[64,1792]{1,0:T(8,128)S(1)}, f32[64,1792]{1,0:T(8,128)}, u32[]{:S(2)}) copy-start(f32[64,1792]{1,0:T(8,128)} %get-tuple-element.20) | copy-start | bytes 1376260
  99.2 4.6 %copy-start.9 = (f32[64,1792]{1,0:T(8,128)S(1)}, f32[64,1792]{1,0:T(8,128)}, u32[]{:S(2)}) copy-start(f32[64,1792]{1,0:T(8,128)} %get-tuple-element.21) | copy-start | bytes 1376260
  106.1 3.6 %copy-start.6 = (bf16[64,1792]{1,0:T(8,128)(2,1)}, bf16[64,1792]{1,0:T(8,128)(2,1)S(1)}, u32[]{:S(2)}) copy-start(bf16[64,1792]{1,0:T(8,128)(2,1)S(1)} %get-tuple-element.31.refs_0_) | copy-start | bytes 688132
  136.1 4.7 %copy-start.1 = (bf16[128,8,1792]{2,0,1:T(8,128)(2,1)S(1)}, bf16[128,8,1792]{2,0,1:T(8,128)(2,1)}, u32[]{:S(2)}) copy-start(bf16[128,8,1792]{2,0,1:T(8,128)(2,1)} %multiply_convert_fusion.5) | copy-start | bytes 11010052
  136.1 4.7 %copy-start.11 = (bf16[4,64,1792]{2,1,0:T(8,128)(2,1)S(1)}, bf16[4,64,1792]{2,1,0:T(8,128)(2,1)}, u32[]{:S(2)}) copy-start(bf16[4,64,1792]{2,1,0:T(8,128)(2,1)} %get-tuple-element.25) | copy-start | bytes 2752516
  140.8 3.9 %copy-start.7 = (bf16[4,64,1792]{2,1,0:T(8,128)(2,1)S(1)}, bf16[4,64,1792]{2,1,0:T(8,128)(2,1)}, u32[]{:S(2)}) copy-start(bf16[4,64,1792]{2,1,0:T(8,128)(2,1)} %get-tuple-element.23) | copy-start | bytes 2752516
  146.7 2.1 %copy-start.5 = (bf16[64,28,1024]{2,0,1:T(8,128)(2,1)S(1)}, bf16[64,28,1024]{2,0,1:T(8,128)(2,1)}, u32[]{:S(2)}) copy-start(bf16[64,28,1024]{2,0,1:T(8,128)(2,1)} %multiply_convert_fusion.3) | copy-start | bytes 11010052
  150.7 25.2 %copy-start.14 = (bf16[8,32,1024]{2,1,0:T(8,128)(2,1)S(1)}, bf16[8,32,1024]{2,1,0:T(8,128)(2,1)}, u32[]{:S(2)}) copy-start(bf16[8,32,1024]{2,1,0:T(8,128)(2,1)} %get-tuple-element.19) | copy-start | bytes 1572868
  175.9 3.6 %copy-start.12 = (bf16[4,64,1792]{2,1,0:T(8,128)(2,1)S(1)}, bf16[4,64,1792]{2,1,0:T(8,128)(2,1)}, u32[]{:S(2)}) copy-start(bf16[4,64,1792]{2,1,0:T(8,128)(2,1)} %get-tuple-element.25) | copy-start | bytes 2752516
  179.6 3.7 %copy-start.10 = (bf16[4,64,1792]{2,1,0:T(8,128)(2,1)S(1)}, bf16[4,64,1792]{2,1,0:T(8,128)(2,1)}, u32[]{:S(2)}) copy-start(bf16[4,64,1792]{2,1,0:T(8,128)(2,1)} %get-tuple-element.26) | copy-start | bytes 2752516
where the time goes:
time: 187 us
  Pallas kernels  95.1 us (51%)
  matrix products  54.2 us (29%)
  other arithmetic  25.1 us (13%)
  local copies, waits for them, and re-layouts  11.4 us (6%)
    pallas_call x2, Pallas kernels, gather(): pl.pallas_call(functools.partial(gather_kernel, axis, n, inner, nx, ny, c...  50.8 us
    pallas_call x2, Pallas kernels, scatter(): pl.pallas_call(functools.partial(scatter_kernel, axis, n, inner, count),...  44.3 us
    dot_general x3, matrix products, rotate_rows(): jnp.einsum('kl,bkc->blc', table.astype(jnp.bfloat16), blocks, preferred_e...  16.3 us
    another operation x3, other arithmetic  14.2 us
    dot_general x3, matrix products, contract_rows(): lax.dot_general(left_mat, right_mat, (((0,), (0,)), ((), ())), preferred_...  10.8 us
    dot_general x3, matrix products, contract_cols(): lax.dot_general(left_mat, right_mat, (((1,), (1,)), ((), ())), preferred_...  9.78 us
    dot_general x6, matrix products, rotate_cols(): jnp.einsum('rbk,kl->rbl', blocks, table.astype(jnp.bfloat16), preferred_e...  6.61 us
    select_n x3, other arithmetic, peak_tile(): tile = jnp.where(rows == i, value, tile)  4.59 us

commit v1 on v0

v1 whole, which is shorter than its diff:
```python
import functools

import jax
import jax.numpy as jnp
from jax import lax
from jax.experimental import pallas as pl
from jax.experimental.pallas import tpu as pltpu
from jax.sharding import PartitionSpec as P

ROT_BLOCK = 128
HID_BLOCK = 64
CORES = 2

fp_top = 448.0
tiny = 1e-06

MESH = pl.DeviceIdType.MESH
VMEM = pl.BlockSpec(memory_space=pltpu.VMEM)
ANY = pl.BlockSpec(memory_space=pl.ANY)
DMA = pltpu.SemaphoreType.DMA
F32 = jnp.float32
BF16 = jnp.bfloat16


def rot_table(size, block):
    shift = block.bit_length() - 1
    row = lax.broadcasted_iota(jnp.int32, (size, size), 0)
    col = lax.broadcasted_iota(jnp.int32, (size, size), 1)
    bits = row & col & (block - 1)
    bits = bits ^ (bits >> 4)
    bits = bits ^ (bits >> 2)
    bits = bits ^ (bits >> 1)
    sign = 1 - 2 * (bits & 1)
    return jnp.where((row >> shift) == (col >> shift), sign, 0).astype(F32).astype(BF16)


def dot(left, right):
    return jnp.dot(left, right, preferred_element_type=F32)


def dot_t(left, right):
    return lax.dot_general(
        left, right, (((1,), (1,)), ((), ())), preferred_element_type=F32
    )


def dot_wide(values, table):
    high = values.astype(BF16)
    rest = values - high.astype(F32)
    mid = rest.astype(BF16)
    low = (rest - mid.astype(F32)).astype(BF16)
    return dot(high, table) + (dot(mid, table) + dot(low, table))


def remote(src, dst, send, recv, target):
    return pltpu.make_async_remote_copy(
        src_ref=src, dst_ref=dst, send_sem=send, recv_sem=recv,
        device_id=target, device_id_type=MESH,
    )


def loop(low, high, body):
    def step(i, carry):
        body(i)
        return carry
    lax.fori_loop(low, high, step, 0)


def greet(n, me, axis):
    barrier = pltpu.get_barrier_semaphore()

    def hello(k):
        pl.semaphore_signal(
            barrier, inc=1, device_id={axis: lax.rem(me + k, n)}, device_id_type=MESH
        )

    loop(1, n, hello)


def exchange(n, me, axis, src, slots, send, recv):
    def copy(k, slot):
        return remote(
            src, slots.at[slot], send.at[k], recv.at[k], {axis: lax.rem(me + k, n)}
        )

    def start(k):
        copy(k, me).start()

    def finish(k):
        copy(k, lax.rem(me + n - k, n)).wait()

    return (lambda: loop(1, n, start)), (lambda: loop(1, n, finish))


def fold(values):
    rows, cols = values.shape
    return jnp.max(jnp.abs(values).reshape(rows // 8, 8, cols), axis=0)


def ds(i, size):
    return pl.ds(pl.multiple_of(i * size, size), size)


def peak_tile(values):
    rows = lax.broadcasted_iota(jnp.int32, (8, 128), 0)
    tile = jnp.full((8, 128), values[0], F32)
    for i, value in enumerate(values[1:], 1):
        tile = jnp.where(rows == i, value, tile)
    return tile


def tile_scalar(tile, i):
    return jnp.max(tile[i : i + 1, :])


def layer_kernel(dims, names, *refs):
    nx, ny, lanes, tl, wide, hid, piece, band = dims
    r = dict(zip(names, refs))
    total_t = tl * ny
    tc = total_t // nx
    nc = hid // piece
    nb = wide // band
    gx, gy = lax.axis_index("gx"), lax.axis_index("gy")
    tok_s, hid_s = ROT_BLOCK ** (-0.5), HID_BLOCK ** (-0.5)

    wg, wu, wd = r["wg"], r["wu"], r["wd"]
    gate_hbm, up_hbm, down_hbm = r["gate"], r["up"], r["down"]

    def load(i, c):
        cols = ds(c, piece)
        src, dst = [
            (gate_hbm.at[:, cols], wg.at[c]),
            (up_hbm.at[:, cols], wu.at[c]),
            (down_hbm.at[cols, :], wd.at[c]),
        ][i]
        return pltpu.make_async_copy(src, dst, r["load"].at[i, c])

    def start_loads(c):
        for i in range(3):
            load(i, c).start()

    loop(0, nc, start_loads)
    greet(nx, gx, "gx")
    greet(ny, gy, "gy")
    pl.semaphore_wait(pltpu.get_barrier_semaphore(), nx - 1 + ny - 1)

    g_outer = ny // lanes
    g_hi, g_lo = gy // lanes, lax.rem(gy, lanes)
    g_blocks, g_all = [r["tokens"], r["cot"]], [r["all_tok"], r["all_cot"]]

    def g_far(i, k, slot):
        j = lax.rem(g_hi + k, g_outer)
        return remote(
            g_blocks[i], g_all[i].at[slot], r["g_sf"].at[i, k], r["g_rf"].at[i, k],
            {"gy": lanes * j + g_lo},
        )

    def g_near(i, k, o, src, slot):
        return remote(
            src, g_all[i].at[slot], r["g_sn"].at[i, k, o], r["g_rn"].at[i, k, o],
            {"gy": lanes * g_hi + lax.rem(g_lo + o, lanes)},
        )

    for i in range(2):
        for k in range(1, g_outer):
            g_far(i, k, gy).start()
        for o in range(1, lanes):
            g_near(i, 0, o, g_blocks[i], gy).start()

    def g_forward(k):
        mine = lanes * lax.rem(g_hi + g_outer - k, g_outer) + g_lo
        for i in range(2):
            g_far(i, k, mine).wait()
            for o in range(1, lanes):
                g_near(i, k, o, g_all[i].at[mine], mine).start()

    def g_finish(i):
        for o in range(1, lanes):
            side = lax.rem(g_lo + lanes - o, lanes)
            g_near(i, 0, o, g_blocks[i], lanes * g_hi + side).wait()
            for k in range(1, g_outer):
                row = lanes * lax.rem(g_hi + g_outer - k, g_outer)
                g_near(i, k, o, g_all[i].at[row + g_lo], row + side).wait()

    r["tab_w"][...] = rot_table(band, ROT_BLOCK)
    r["tab_h"][...] = rot_table(piece, HID_BLOCK)
    for i in range(2):
        g_all[i][gy] = g_blocks[i][...]
    tok_top = jnp.zeros((8, band), F32)
    for b in range(nb):
        cols = slice(b * band, (b + 1) * band)
        tok_top = jnp.maximum(tok_top, fold(dot(r["tokens"][:, cols], r["tab_w"][...])))

    def peak_step(c, tops):
        gate_top, up_top, down_top = tops
        for i in range(3):
            load(i, c).wait()
        for b in range(nb):
            rows = slice(b * band, (b + 1) * band)
            gate_top = jnp.maximum(gate_top, fold(dot(r["tab_w"][...], wg[c, rows, :])))
            up_top = jnp.maximum(up_top, fold(dot(r["tab_w"][...], wu[c, rows, :])))
            down_top = jnp.maximum(down_top, fold(dot(r["tab_h"][...], wd[c, :, rows])))
        return gate_top, up_top, down_top

    tops = (
        jnp.zeros((8, piece), F32), jnp.zeros((8, piece), F32), jnp.zeros((8, band), F32)
    )
    tops = lax.fori_loop(0, nc, peak_step, tops)
    r["tile"][...] = peak_tile([
        jnp.max(tok_top) * tok_s, jnp.max(tops[0]) * tok_s,
        jnp.max(tops[1]) * tok_s, jnp.max(tops[2]) * hid_s,
    ])
    start_x, finish_x = exchange(nx, gx, "gx", r["tile"], r["slots_x"], r["p_sx"], r["p_rx"])
    start_y, finish_y = exchange(ny, gy, "gy", r["mid"], r["slots_y"], r["p_sy"], r["p_ry"])
    start_x()
    r["slots_x"][gx] = r["tile"][...]
    loop(1, g_outer, g_forward)
    finish_x()
    r["mid"][...] = jnp.max(r["slots_x"][...], axis=0)
    start_y()
    r["slots_y"][gy] = r["mid"][...]
    g_finish(0)
    finish_y()
    top = jnp.max(r["slots_y"][...], axis=0)
    inverse = 1.0 / (top + tiny)
    unit = top / fp_top
    pair = top[0:1, :] * top / (fp_top * fp_top)
    tok_inv = tile_scalar(inverse, 0) * tok_s
    gate_inv = tile_scalar(inverse, 1) * tok_s
    up_inv = tile_scalar(inverse, 2) * tok_s
    down_inv = tile_scalar(inverse, 3) * hid_s
    tok_unit, gate_unit, up_unit, down_unit = (tile_scalar(unit, i) for i in range(4))
    gate_scale, up_scale = tile_scalar(pair, 1), tile_scalar(pair, 2)

    def soft(values):
        return (fp_top * jnp.tanh(values)).astype(BF16)

    for b in range(nb):
        cols = slice(b * band, (b + 1) * band)
        raw = r["all_tok"][:, :, cols].reshape(total_t, band)
        r["tok"][:, cols] = soft(dot(raw, r["tab_w"][...]) * tok_inv)

    def cast_step(c):
        for b in range(nb):
            rows = slice(b * band, (b + 1) * band)
            wg[c, rows, :] = soft(dot(r["tab_w"][...], wg[c, rows, :]) * gate_inv)
            wu[c, rows, :] = soft(dot(r["tab_w"][...], wu[c, rows, :]) * up_inv)
            wd[c, :, rows] = soft(dot(r["tab_h"][...], wd[c, :, rows]) * down_inv)

    x_outer = nx // CORES
    x_hi, x_lo = gx // CORES, lax.rem(gx, CORES)
    x_order = list(range(1, x_outer)) + [0]
    part, first, second, third, act = (
        r["part"], r["first"], r["second"], r["third"], r["act"]
    )

    def s_near(c, k, o):
        j, to = lax.rem(x_hi + k, x_outer), lax.rem(x_lo + o, CORES)
        return remote(
            part.at[c, CORES * j + to], first.at[c, k, o - 1], r["s_s1"].at[c, k, o],
            r["s_r1"].at[c, k, o], {"gx": CORES * x_hi + to},
        )

    def s_far(c, k):
        j = lax.rem(x_hi + k, x_outer)
        return remote(
            second.at[c, k - 1], third.at[c, k - 1], r["s_s2"].at[c, k],
            r["s_r2"].at[c, k], {"gx": CORES * j + x_lo},
        )

    def a_far(c, k, slot):
        j = lax.rem(x_hi + k, x_outer)
        return remote(
            act.at[c, slot], act.at[c, slot], r["a_sf"].at[c, k], r["a_rf"].at[c, k],
            {"gx": CORES * j + x_lo},
        )

    def a_near(c, k, o, slot):
        return remote(
            act.at[c, slot], act.at[c, slot], r["a_sn"].at[c, k, o], r["a_rn"].at[c, k, o],
            {"gx": CORES * x_hi + lax.rem(x_lo + o, CORES)},
        )

    def matmul_step(c):
        for i in range(3):
            if i == 2:
                total = dot_t(r["all_cot"][...].reshape(total_t, wide), wd[c])
            else:
                total = dot(r["tok"][...], (wg, wu)[i][c])
            part[c, :, i] = total.reshape(nx, tc, piece)
        for k in x_order:
            for o in range(1, CORES):
                s_near(c, k, o).start()

    def near_sum(c, k, i):
        total = part[c, CORES * lax.rem(x_hi + k, x_outer) + x_lo, i]
        for o in range(1, CORES):
            total = total + first[c, k, o - 1, i]
        return total

    def pass_step(c):
        for k in x_order[:-1]:
            for o in range(1, CORES):
                s_near(c, k, o).wait()
            for i in range(3):
                second[c, k - 1, i] = near_sum(c, k, i).astype(BF16)
            s_far(c, k).start()

    def act_step(c):
        for o in range(1, CORES):
            s_near(c, 0, o).wait()
        for k in x_order[:-1]:
            s_far(c, k).wait()

        def full(i):
            total = near_sum(c, 0, i)
            for k in x_order[:-1]:
                total = total + third[c, k - 1, i].astype(F32)
            return total

        gate_pre = full(0) * gate_scale
        up_pre = full(1) * up_scale
        sig = jax.nn.sigmoid(gate_pre)
        hidden = (gate_pre * sig * up_pre).astype(BF16)
        act[c, gx, 0] = hidden
        grad = dot_wide(full(2) * down_unit, r["tab_h"][...]) * hid_s
        act[c, gx, 1] = (
            grad * up_pre * sig * (1.0 + gate_pre * (1.0 - sig))
        ).astype(BF16)
        act[c, gx, 2] = (grad * gate_pre * sig).astype(BF16)
        for k in range(1, x_outer):
            a_far(c, k, gx).start()
        for o in range(1, CORES):
            a_near(c, 0, o, gx).start()
        r["top_h"][...] = jnp.maximum(
            r["top_h"][...], fold(dot(hidden, r["tab_h"][...]))
        )

    def forward_step(c):
        for k in range(1, x_outer):
            mine = CORES * lax.rem(x_hi + x_outer - k, x_outer) + x_lo
            a_far(c, k, mine).wait()
            for o in range(1, CORES):
                a_near(c, k, o, mine).start()

    def arrive_step(c):
        for o in range(1, CORES):
            side = lax.rem(x_lo + CORES - o, CORES)
            for k in range(x_outer):
                row = CORES * lax.rem(x_hi + x_outer - k, x_outer)
                a_near(c, k, o, row + side).wait()

    r["top_h"][...] = jnp.zeros((8, piece), F32)
    cast_step(0)
    g_finish(1)

    def pipeline(i):
        @pl.when(i < nc)
        def _():
            matmul_step(i)

        @pl.when(i + 1 < nc)
        def _():
            cast_step(i + 1)

        @pl.when(i < nc)
        def _():
            pass_step(i)

        @pl.when((i >= 1) & (i < nc + 1))
        def _():
            act_step(i - 1)

        @pl.when(i >= 2)
        def _():
            forward_step(i - 2)

    loop(0, nc + 2, pipeline)

    r["tile2"][...] = peak_tile([jnp.max(r["top_h"][...]) * hid_s])
    start_y2, finish_y2 = exchange(
        ny, gy, "gy", r["tile2"], r["slots_y2"], r["q_sy"], r["q_ry"]
    )
    start_x2, finish_x2 = exchange(
        nx, gx, "gx", r["mid2"], r["slots_x2"], r["q_sx"], r["q_rx"]
    )
    start_y2()
    r["slots_y2"][gy] = r["tile2"][...]
    loop(0, nc, arrive_step)

    y_outer = ny // lanes
    y_order = list(range(1, y_outer)) + [0]
    bufs = [r["out_part"], r["in_part"]]
    ones, twos, threes = r["y_one"], r["y_two"], r["y_three"]

    def y_near(i, k, o):
        j, to = lax.rem(g_hi + k, y_outer), lax.rem(g_lo + o, lanes)
        return remote(
            bufs[i].at[lanes * j + to], ones.at[i, k, o - 1], r["y_s1"].at[i, k, o],
            r["y_r1"].at[i, k, o], {"gy": lanes * g_hi + to},
        )

    def y_far(i, k):
        j = lax.rem(g_hi + k, y_outer)
        return remote(
            twos.at[i, k - 1], threes.at[i, k - 1], r["y_s2"].at[i, k],
            r["y_r2"].at[i, k], {"gy": lanes * j + g_lo},
        )

    def y_send(i):
        for k in y_order:
            for o in range(1, lanes):
                y_near(i, k, o).start()

    def y_sum(i, k):
        total = bufs[i][lanes * lax.rem(g_hi + k, y_outer) + g_lo].astype(F32)
        for o in range(1, lanes):
            total = total + ones[i, k, o - 1].astype(F32)
        return total

    def y_pass(i, k):
        for o in range(1, lanes):
            y_near(i, k, o).wait()
        twos[i, k - 1] = y_sum(i, k).astype(BF16)
        y_far(i, k).start()

    def y_close(i):
        for o in range(1, lanes):
            y_near(i, 0, o).wait()
        total = y_sum(i, 0)
        for k in y_order[:-1]:
            y_far(i, k).wait()
            total = total + threes[i, k - 1].astype(F32)
        return total

    def rows_of(c, i):
        return act[c, :, i].reshape(total_t, piece)

    def in_step(b):
        rows = ds(b, band)
        gate_sum = jnp.zeros((total_t, band), F32)
        up_sum = jnp.zeros((total_t, band), F32)
        for c in range(nc):
            gate_sum = gate_sum + dot_t(rows_of(c, 1), wg[c, rows, :])
            up_sum = up_sum + dot_t(rows_of(c, 2), wu[c, rows, :])
        total = gate_sum * gate_unit + up_sum * up_unit
        r["in_part"][:, :, rows] = total.astype(BF16).reshape(ny, tl, band)

    loop(0, nb, in_step)
    y_send(1)
    finish_y2()
    r["mid2"][...] = jnp.max(r["slots_y2"][...], axis=0)
    start_x2()
    r["slots_x2"][gx] = r["mid2"][...]

    for b in range(nb):
        cols = slice(b * band, (b + 1) * band)
        turned = dot(r["tok"][:, cols], r["tab_w"][...]) * tok_s
        r["tok_t"][cols, :] = turned.T.astype(BF16)

    gate_out, up_out, down_out = r["gate_grad"], r["up_grad"], r["down_grad"]

    def store(i, c):
        cols = ds(c, piece)
        src, dst = [
            (wg.at[c], gate_out.at[:, cols]),
            (wu.at[c], up_out.at[:, cols]),
            (wd.at[c], down_out.at[cols, :]),
        ][i]
        return pltpu.make_async_copy(src, dst, r["save"].at[i, c])

    def weight_grads(c):
        for b in range(nb):
            rows = slice(b * band, (b + 1) * band)
            wg[c, rows, :] = (
                dot(r["tok_t"][rows, :], rows_of(c, 1)) * tok_unit
            ).astype(BF16)
            wu[c, rows, :] = (
                dot(r["tok_t"][rows, :], rows_of(c, 2)) * tok_unit
            ).astype(BF16)
        store(0, c).start()
        store(1, c).start()

    finish_x2()
    top2 = jnp.max(r["slots_x2"][...], axis=0)
    hidden_inv = tile_scalar(1.0 / (top2 + tiny), 0) * hid_s
    hidden_unit = tile_scalar(top2 / fp_top, 0)
    out_scale = tile_scalar(top2[0:1, :] * top[3:4, :] / (fp_top * fp_top), 0)

    def hidden_step(c):
        r["hid"][c] = soft(dot(rows_of(c, 0), r["tab_h"][...]) * hidden_inv)

    loop(0, nc, hidden_step)

    def out_step(b):
        cols = ds(b, band)
        total = jnp.zeros((total_t, band), F32)
        for c in range(nc):
            total = total + dot(r["hid"][c], wd[c, :, cols])
        r["out_part"][:, :, cols] = total.astype(BF16).reshape(ny, tl, band)

    loop(0, nb, out_step)
    y_send(0)

    def down_grads(c):
        turned = (dot(r["hid"][c], r["tab_h"][...]) * hid_s).T.astype(BF16)
        cot = r["all_cot"][...].reshape(total_t, wide)
        wd[c] = (dot(turned, cot) * hidden_unit).astype(BF16)
        store(2, c).start()

    cuts = [nc * k // y_outer for k in range(y_outer + 1)]
    for n, k in enumerate(y_order):
        loop(cuts[n], cuts[n + 1], weight_grads)
        if k:
            y_pass(1, k)
    for n, k in enumerate(y_order):
        loop(cuts[n], cuts[n + 1], down_grads)
        if k:
            y_pass(0, k)

    total = y_close(1)
    for b in range(nb):
        cols = slice(b * band, (b + 1) * band)
        r["input_grad"][:, cols] = (
            dot_wide(total[:, cols], r["tab_w"][...]) * tok_s
        ).astype(BF16)
    r["output"][...] = (y_close(0) * out_scale).astype(BF16)

    def drain(c):
        for i in range(3):
            store(i, c).wait()

    loop(0, nc, drain)


def shards(nx, ny, tokens, cotangent, gate_weight, up_weight, down_weight):
    lanes = 1 << max((ny.bit_length() - 2) // 2, 0)
    tl, wide = tokens.shape
    hid = gate_weight.shape[1]
    piece = 256 if hid % 256 == 0 else hid
    band = 256 if wide % 256 == 0 else wide
    nc = hid // piece
    total_t = tl * ny
    tc = total_t // nx
    x_outer, y_outer = nx // CORES, ny // lanes
    dims = (nx, ny, lanes, tl, wide, hid, piece, band)
    ins = ["tokens", "cot", "gate", "up", "down"]
    outs = ["output", "input_grad", "gate_grad", "up_grad", "down_grad"]
    tile = pltpu.VMEM((8, 128), F32)
    scratch = {
        "wg": pltpu.VMEM((nc, wide, piece), BF16),
        "wu": pltpu.VMEM((nc, wide, piece), BF16),
        "wd": pltpu.VMEM((nc, piece, wide), BF16),
        "load": DMA((3, nc)),
        "save": DMA((3, nc)),
        "all_tok": pltpu.VMEM((ny, tl, wide), BF16),
        "all_cot": pltpu.VMEM((ny, tl, wide), BF16),
        "g_sf": DMA((2, y_outer)), "g_rf": DMA((2, y_outer)),
        "g_sn": DMA((2, y_outer, lanes)), "g_rn": DMA((2, y_outer, lanes)),
        "tab_w": pltpu.VMEM((band, band), BF16),
        "tab_h": pltpu.VMEM((piece, piece), BF16),
        "tile": tile, "mid": tile, "tile2": tile, "mid2": tile,
        "slots_x": pltpu.VMEM((nx, 8, 128), F32),
        "slots_y": pltpu.VMEM((ny, 8, 128), F32),
        "slots_x2": pltpu.VMEM((nx, 8, 128), F32),
        "slots_y2": pltpu.VMEM((ny, 8, 128), F32),
        "p_sx": DMA((nx,)), "p_rx": DMA((nx,)), "p_sy": DMA((ny,)), "p_ry": DMA((ny,)),
        "q_sx": DMA((nx,)), "q_rx": DMA((nx,)), "q_sy": DMA((ny,)), "q_ry": DMA((ny,)),
        "tok": pltpu.VMEM((total_t, wide), BF16),
        "tok_t": pltpu.VMEM((wide, total_t), BF16),
        "part": pltpu.VMEM((nc, nx, 3, tc, piece), F32),
        "first": pltpu.VMEM((nc, x_outer, CORES - 1, 3, tc, piece), F32),
        "second": pltpu.VMEM((nc, x_outer - 1, 3, tc, piece), BF16),
        "third": pltpu.VMEM((nc, x_outer - 1, 3, tc, piece), BF16),
        "act": pltpu.VMEM((nc, nx, 3, tc, piece), BF16),
        "hid": pltpu.VMEM((nc, total_t, piece), BF16),
        "s_s1": DMA((nc, x_outer, CORES)), "s_r1": DMA((nc, x_outer, CORES)),
        "s_s2": DMA((nc, x_outer)), "s_r2": DMA((nc, x_outer)),
        "a_sf": DMA((nc, x_outer)), "a_rf": DMA((nc, x_outer)),
        "a_sn": DMA((nc, x_outer, CORES)), "a_rn": DMA((nc, x_outer, CORES)),
        "top_h": pltpu.VMEM((8, piece), F32),
        "out_part": pltpu.VMEM((ny, tl, wide), BF16),
        "in_part": pltpu.VMEM((ny, tl, wide), BF16),
        "y_one": pltpu.VMEM((2, y_outer, lanes - 1, tl, wide), BF16),
        "y_two": pltpu.VMEM((2, y_outer - 1, tl, wide), BF16),
        "y_three": pltpu.VMEM((2, y_outer - 1, tl, wide), BF16),
        "y_s1": DMA((2, y_outer, lanes)), "y_r1": DMA((2, y_outer, lanes)),
        "y_s2": DMA((2, y_outer)), "y_r2": DMA((2, y_outer)),
    }
    names = tuple(ins + outs + list(scratch))
    small = jax.ShapeDtypeStruct(tokens.shape, BF16)
    return pl.pallas_call(
        functools.partial(layer_kernel, dims, names),
        out_shape=[small, small] + [
            jax.ShapeDtypeStruct(w.shape, BF16)
            for w in (gate_weight, up_weight, down_weight)
        ],
        in_specs=[VMEM, VMEM, ANY, ANY, ANY],
        out_specs=[VMEM, VMEM, ANY, ANY, ANY],
        scratch_shapes=list(scratch.values()),
        compiler_params=pltpu.CompilerParams(
            collective_id=0, has_side_effects=True, vmem_limit_bytes=62 * 2 ** 20
        ),
    )(tokens, cotangent, gate_weight, up_weight, down_weight)


def solution(mesh):
    in_specs = (P("gy", "gx"), P("gy", "gx"), P("gx", "gy"), P("gx", "gy"), P("gy", "gx"))
    out_specs = (P("gy", "gx"), P("gy", "gx"), P("gx", "gy"), P("gx", "gy"), P("gy", "gx"))
    nx, ny = mesh.shape["gx"], mesh.shape["gy"]
    return jax.shard_map(
        functools.partial(shards, nx, ny),
        mesh=mesh, in_specs=in_specs, out_specs=out_specs, check_vma=False,
    )
```

time: 187 us -> 100 us (0.53)
  matrix products: 54.2 us -> 0 us
  other arithmetic: 25.1 us -> 0 us
  Pallas kernels: 95.1 us -> 86.8 us
    dot_general x20 -> x0, matrix products: 54.2 us -> none  [the longest x3 16.3 us: rotate_rows(): jnp.einsum('kl,bkc->blc', table.astype(jnp.bfloat16), blocks, preferred_e...]
    another operation x3 -> x0, other arithmetic: 14.2 us -> none
    unnamed x41 -> x9, local copies, waits for them, and re-layouts: 2.96 us -> 12.4 us
    pallas_call x4 -> x1, Pallas kernels: 95.1 us -> 86.8 us  [shards(): pl.pallas_call(functools.partial(layer_kernel, dims, names), out_shape=[s...]
    select_n x3 -> x0, other arithmetic: 4.59 us -> none  [peak_tile(): tile = jnp.where(rows == i, value, tile)]
    convert_element_type x2 -> x0, other arithmetic: 4.47 us -> none  [the longest x1 2.28 us: shards(): up_act = (hidden_grad * gate_pre * sigmoid_gate).astype(jnp.bfloat16)]
    slice x2 -> x0, local copies, waits for them, and re-layouts: 3.18 us -> none  [the longest x1 1.98 us: shards(): peaks[2, i, 0]]
    another operation x1 -> x0, local copies, waits for them, and re-layouts: 2.02 us -> none  [rotate_cols(): blocks = matrix.reshape(row_total, col_total // block_size, block_size)]
where the time goes in v1:
time: 100 us; the launch traced here: 99.9 us
  Pallas kernels  86.8 us (87%)
  local copies, waits for them, and re-layouts  12.4 us (12%)
    pallas_call x1, Pallas kernels, shards(): pl.pallas_call(functools.partial(layer_kernel, dims, names), out_shape=[s...  86.8 us
    unnamed x9, local copies, waits for them, and re-layouts  12.4 us

profile of v1, /device:TPU:0, one launch (start us, length us, event | category | flops | bytes accessed | tf_op | source)
XLA Modules:
  0.0 99.9 jit_solution(10224794830277647802)
XLA Ops:
  0.6 86.8 %shard_map.92 = (bf16[32,1024]{1,0:T(8,128)(2,1)}, bf16[32,1024]{1,0:T(8,128)(2,1)}, bf16[1024,1792]{1,0:T(8,128)(2,1)}, bf16[1024,1792]{1,0:T(8,128)(2,1)}, bf16[1792,1024]{1,0:T(8,128)(2,1)}) custom-call(bf16[32,1024]{1,0:T(8,128)(2,1)} %refs_0_.1, bf16[32,1024]{1,0:T(8,128)(2,1)} %refs_1_.1, bf16[1024,1792]{1,0:T(8,128)(2,1)} %refs_2_.1, ...), custom_call_target="tpu_custom_call" | custom-call | tf_op jit(solution)/shard_map/pallas_call | solution.py:592
  87.5 1.5 %copy.15 = bf16[32,1024]{1,0:T(8,128)(2,1)} copy(bf16[32,1024]{1,0:T(8,128)(2,1)} %get-tuple-element.10) | data formatting | bytes 131072
  88.9 1.5 %copy.16 = bf16[32,1024]{1,0:T(8,128)(2,1)} copy(bf16[32,1024]{1,0:T(8,128)(2,1)} %get-tuple-element.11) | data formatting | bytes 131072
  90.4 0.0 copy-start.1
  90.4 4.3 %copy.17 = bf16[1024,1792]{1,0:T(8,128)(2,1)} copy(bf16[1024,1792]{1,0:T(8,128)(2,1)} %get-tuple-element.12) | data formatting | bytes 7340032
  94.7 0.0 copy-done.1
  94.7 0.0 copy-start
  94.7 1.9 %copy.18 = bf16[1024,1792]{1,0:T(8,128)(2,1)} copy(bf16[1024,1792]{1,0:T(8,128)(2,1)S(1)} %copy-done.1) | data formatting | bytes 7340032
  96.6 1.5 %copy-done = bf16[1792,1024]{1,0:T(8,128)(2,1)S(1)} copy-done((bf16[1792,1024]{1,0:T(8,128)(2,1)S(1)}, bf16[1792,1024]{1,0:T(8,128)(2,1)}, u32[]{:S(2)}) %copy-start) | copy-done | bytes 3670040
  98.0 1.8 %copy.19 = bf16[1792,1024]{1,0:T(8,128)(2,1)} copy(bf16[1792,1024]{1,0:T(8,128)(2,1)S(1)} %copy-done) | data formatting | bytes 7340032
Async XLA Ops:
  90.4 4.3 %copy-start.1 = (bf16[1024,1792]{1,0:T(8,128)(2,1)S(1)}, bf16[1024,1792]{1,0:T(8,128)(2,1)}, u32[]{:S(2)}) copy-start(bf16[1024,1792]{1,0:T(8,128)(2,1)} %get-tuple-element.13) | copy-start | bytes 11010052
  94.7 3.4 %copy-start = (bf16[1792,1024]{1,0:T(8,128)(2,1)S(1)}, bf16[1792,1024]{1,0:T(8,128)(2,1)}, u32[]{:S(2)}) copy-start(bf16[1792,1024]{1,0:T(8,128)(2,1)} %get-tuple-element.14) | copy-start | bytes 11010052

commit v2 on v1

v2 whole, which is shorter than its diff:
```python
import functools

import jax
import jax.numpy as jnp
from jax import lax
from jax.experimental import pallas as pl
from jax.experimental.pallas import tpu as pltpu
from jax.sharding import PartitionSpec as P

ROT_BLOCK = 128
HID_BLOCK = 64
CORES = 2
VMEM_MIB = 50
STORE_MIB = 12
LAG = 2

fp_top = 448.0
tiny = 1e-06

MESH = pl.DeviceIdType.MESH
VMEM = pl.BlockSpec(memory_space=pltpu.VMEM)
HBM = pl.BlockSpec(memory_space=pltpu.HBM)
DMA = pltpu.SemaphoreType.DMA
F32 = jnp.float32
BF16 = jnp.bfloat16


def rot_table(size, block):
    shift = block.bit_length() - 1
    row = lax.broadcasted_iota(jnp.int32, (size, size), 0)
    col = lax.broadcasted_iota(jnp.int32, (size, size), 1)
    bits = row & col & (block - 1)
    bits = bits ^ (bits >> 4)
    bits = bits ^ (bits >> 2)
    bits = bits ^ (bits >> 1)
    sign = 1 - 2 * (bits & 1)
    return jnp.where((row >> shift) == (col >> shift), sign, 0).astype(F32).astype(BF16)


def dot(left, right):
    return jnp.dot(left, right, preferred_element_type=F32)


def dot_t(left, right):
    return lax.dot_general(
        left, right, (((1,), (1,)), ((), ())), preferred_element_type=F32
    )


def dot_wide(values, table):
    high = values.astype(BF16)
    rest = values - high.astype(F32)
    mid = rest.astype(BF16)
    low = (rest - mid.astype(F32)).astype(BF16)
    return dot(high, table) + (dot(mid, table) + dot(low, table))


def remote(src, dst, send, recv, target):
    return pltpu.make_async_remote_copy(
        src_ref=src, dst_ref=dst, send_sem=send, recv_sem=recv,
        device_id=target, device_id_type=MESH,
    )


def loop(low, high, body):
    def step(i, carry):
        body(i)
        return carry
    lax.fori_loop(low, high, step, 0)


def greet(n, me, axis):
    barrier = pltpu.get_barrier_semaphore()

    def hello(k):
        pl.semaphore_signal(
            barrier, inc=1, device_id={axis: lax.rem(me + k, n)}, device_id_type=MESH
        )

    loop(1, n, hello)


def take(ref, sem):
    pltpu.make_async_copy(ref, ref, sem).wait()


def exchange(n, me, axis, src, slots, sems):
    def start(k):
        target = {axis: lax.rem(me + k, n)}
        remote(src, slots.at[k], sems.at[0], sems.at[1], target).start()

    def finish():
        rest = slots.at[pl.ds(1, n - 1)]
        take(rest, sems.at[0])
        take(rest, sems.at[1])

    return (lambda: loop(1, n, start)), finish


def fold(values):
    rows, cols = values.shape
    return jnp.max(jnp.abs(values).reshape(rows // 8, 8, cols), axis=0)


def ds(i, size):
    return pl.ds(pl.multiple_of(i * size, size), size)


def peak_tile(values):
    rows = lax.broadcasted_iota(jnp.int32, (8, 128), 0)
    tile = jnp.full((8, 128), values[0], F32)
    for i, value in enumerate(values[1:], 1):
        tile = jnp.where(rows == i, value, tile)
    return tile


def tile_scalar(tile, i):
    return jnp.max(tile[i : i + 1, :])


def layer_kernel(dims, names, *refs):
    nx, ny, lanes, tl, wide, hid, piece, band = dims
    r = dict(zip(names, refs))
    total_t = tl * ny
    tc = total_t // nx
    nc = hid // piece
    nb = wide // band
    gx, gy = lax.axis_index("gx"), lax.axis_index("gy")
    tok_s, hid_s = ROT_BLOCK ** (-0.5), HID_BLOCK ** (-0.5)
    wg, wu, wd = r["wg"], r["wu"], r["wd"]
    all_tok, all_cot = r["all_tok"], r["all_cot"]

    def own_load(i):
        src, dst = ((r["tokens"], all_tok), (r["cot"], all_cot))[i]
        return pltpu.make_async_copy(src, dst.at[gy], r["own"].at[i])

    own_load(0).start()
    own_load(1).start()
    greet(nx, gx, "gx")
    greet(ny, gy, "gy")

    def load(i, c):
        cols = ds(c, piece)
        src, dst = [
            (r["gate"].at[:, cols], wg.at[c]),
            (r["up"].at[:, cols], wu.at[c]),
            (r["down"].at[cols, :], wd.at[c]),
        ][i]
        return pltpu.make_async_copy(src, dst, r["load"].at[i, c])

    def start_loads(c):
        for i in range(3):
            load(i, c).start()

    loop(0, nc, start_loads)
    r["tab_w"][...] = rot_table(band, ROT_BLOCK)
    r["tab_h"][...] = rot_table(piece, HID_BLOCK)
    own_load(0).wait()
    own_load(1).wait()
    pl.semaphore_wait(pltpu.get_barrier_semaphore(), nx - 1 + ny - 1)

    y_outer = ny // lanes
    y_hi, y_lo = gy // lanes, lax.rem(gy, lanes)
    g_all = [all_tok, all_cot]

    def g_far(i, k, slot):
        j = lax.rem(y_hi + k, y_outer)
        return remote(
            g_all[i].at[slot], g_all[i].at[slot], r["g_sf"].at[i], r["g_rf"].at[i, k - 1],
            {"gy": lanes * j + y_lo},
        )

    def g_near(i, o, slot):
        return remote(
            g_all[i].at[slot], g_all[i].at[slot], r["g_sn"].at[i],
            r["g_rn"].at[i], {"gy": lanes * y_hi + lax.rem(y_lo + o, lanes)},
        )

    def g_start(i):
        for k in range(1, y_outer):
            g_far(i, k, gy).start()
        for o in range(1, lanes):
            g_near(i, o, gy).start()

    def g_forward(i, k):
        mine = lanes * lax.rem(y_hi + y_outer - k, y_outer) + y_lo
        g_far(i, k, mine).wait_recv()
        for o in range(1, lanes):
            g_near(i, o, mine).start()

    def g_finish(i):
        take(g_all[i].at[pl.ds(0, y_outer * (lanes - 1))], r["g_rn"].at[i])

    def g_drain(i):
        take(g_all[i].at[pl.ds(0, y_outer - 1)], r["g_sf"].at[i])
        take(g_all[i].at[pl.ds(0, y_outer * (lanes - 1))], r["g_sn"].at[i])

    g_start(0)

    tok_top = jnp.zeros((8, band), F32)
    for b in range(nb):
        cols = slice(b * band, (b + 1) * band)
        tok_top = jnp.maximum(tok_top, fold(dot(all_tok[gy, :, cols], r["tab_w"][...])))

    def peak_step(c, tops):
        gate_top, up_top, down_top = tops
        for i in range(3):
            load(i, c).wait()
        for b in range(nb):
            rows = slice(b * band, (b + 1) * band)
            gate_top = jnp.maximum(gate_top, fold(dot(r["tab_w"][...], wg[c, rows, :])))
            up_top = jnp.maximum(up_top, fold(dot(r["tab_w"][...], wu[c, rows, :])))
            down_top = jnp.maximum(down_top, fold(dot(r["tab_h"][...], wd[c, :, rows])))
        return gate_top, up_top, down_top

    tops = (
        jnp.zeros((8, piece), F32), jnp.zeros((8, piece), F32), jnp.zeros((8, band), F32)
    )
    tops = lax.fori_loop(0, nc, peak_step, tops)
    r["tile"][...] = peak_tile([
        jnp.max(tok_top) * tok_s, jnp.max(tops[0]) * tok_s,
        jnp.max(tops[1]) * tok_s, jnp.max(tops[2]) * hid_s,
    ])
    start_x, finish_x = exchange(nx, gx, "gx", r["tile"], r["slots_x"], r["p_x"])
    start_y, finish_y = exchange(ny, gy, "gy", r["mid"], r["slots_y"], r["p_y"])
    start_x()
    r["slots_x"][0] = r["tile"][...]
    for k in range(1, y_outer - 1):
        g_forward(0, k)
    finish_x()
    r["mid"][...] = jnp.max(r["slots_x"][...], axis=0)
    start_y()
    r["slots_y"][0] = r["mid"][...]
    g_forward(0, y_outer - 1)
    g_start(1)
    g_finish(0)
    finish_y()
    top = jnp.max(r["slots_y"][...], axis=0)
    inverse = 1.0 / (top + tiny)
    unit = top / fp_top
    pair = top[0:1, :] * top / (fp_top * fp_top)
    tok_inv = tile_scalar(inverse, 0) * tok_s
    gate_inv = tile_scalar(inverse, 1) * tok_s
    up_inv = tile_scalar(inverse, 2) * tok_s
    down_inv = tile_scalar(inverse, 3) * hid_s
    tok_unit, gate_unit, up_unit, down_unit = (tile_scalar(unit, i) for i in range(4))
    gate_scale, up_scale = tile_scalar(pair, 1), tile_scalar(pair, 2)

    def soft(values):
        return (fp_top * jnp.tanh(values)).astype(BF16)

    for b in range(nb):
        cols = slice(b * band, (b + 1) * band)
        raw = all_tok[:, :, cols].reshape(total_t, band)
        r["tok"][:, cols] = soft(dot(raw, r["tab_w"][...]) * tok_inv)

    def cast_gate_up(c):
        for b in range(nb):
            rows = slice(b * band, (b + 1) * band)
            wg[c, rows, :] = soft(dot(r["tab_w"][...], wg[c, rows, :]) * gate_inv)
            wu[c, rows, :] = soft(dot(r["tab_w"][...], wu[c, rows, :]) * up_inv)

    def cast_down(c):
        for b in range(nb):
            rows = slice(b * band, (b + 1) * band)
            wd[c, :, rows] = soft(dot(r["tab_h"][...], wd[c, :, rows]) * down_inv)

    x_outer = nx // CORES
    x_hi, x_lo = gx // CORES, lax.rem(gx, CORES)
    x_order = list(range(1, x_outer)) + [0]

    class Sums:
        def __init__(self, tag, count):
            self.count = count
            self.part, self.first = r[tag + "_part"], r[tag + "_first"]
            self.second, self.third = r[tag + "_second"], r[tag + "_third"]
            self.s1, self.r1 = r[tag + "_s"].at[0], r[tag + "_r1"]
            self.s2, self.r2 = r[tag + "_s"].at[1], r[tag + "_r2"]

        def near(self, c, k, o):
            j, to = lax.rem(x_hi + k, x_outer), lax.rem(x_lo + o, CORES)
            return remote(
                self.part.at[c, CORES * j + to], self.first.at[c, k, o - 1],
                self.s1, self.r1.at[c, k], {"gx": CORES * x_hi + to},
            )

        def far(self, c, k):
            j = lax.rem(x_hi + k, x_outer)
            return remote(
                self.second.at[c, k - 1], self.third.at[c, k - 1], self.s2,
                self.r2.at[c, k - 1], {"gx": CORES * j + x_lo},
            )

        def send(self, c):
            for k in x_order:
                for o in range(1, CORES):
                    self.near(c, k, o).start()

        def near_sum(self, c, k, i):
            total = self.part[c, CORES * lax.rem(x_hi + k, x_outer) + x_lo, i]
            for o in range(1, CORES):
                total = total + self.first[c, k, o - 1, i]
            return total

        def turn(self, c):
            for k in x_order[:-1]:
                take(self.first.at[c, k], self.r1.at[c, k])
                for i in range(self.count):
                    self.second[c, k - 1, i] = self.near_sum(c, k, i).astype(BF16)
                self.far(c, k).start()

        def close(self, c):
            take(self.first.at[c, 0], self.r1.at[c, 0])
            for k in x_order[:-1]:
                self.far(c, k).wait_recv()

        def drain(self):
            take(self.first, self.s1)
            take(self.third, self.s2)

        def full(self, c, i):
            total = self.near_sum(c, 0, i)
            for k in x_order[:-1]:
                total = total + self.third[c, k - 1, i].astype(F32)
            return total

    class Spread:
        def __init__(self, tag):
            self.act = r[tag]
            self.sf, self.rf = r[tag + "_s"].at[0], r[tag + "_rf"]
            self.sn, self.rn = r[tag + "_s"].at[1], r[tag + "_rn"]

        def far(self, c, k, slot):
            j = lax.rem(x_hi + k, x_outer)
            return remote(
                self.act.at[c, slot], self.act.at[c, slot], self.sf,
                self.rf.at[c, k - 1], {"gx": CORES * j + x_lo},
            )

        def near(self, c, o, slot):
            return remote(
                self.act.at[c, slot], self.act.at[c, slot], self.sn,
                self.rn.at[c], {"gx": CORES * x_hi + lax.rem(x_lo + o, CORES)},
            )

        def send(self, c):
            for k in range(1, x_outer):
                self.far(c, k, gx).start()
            for o in range(1, CORES):
                self.near(c, o, gx).start()

        def forward(self, c):
            for k in range(1, x_outer):
                mine = CORES * lax.rem(x_hi + x_outer - k, x_outer) + x_lo
                self.far(c, k, mine).wait_recv()
                for o in range(1, CORES):
                    self.near(c, o, mine).start()

        def arrive(self, c):
            take(self.act.at[c, pl.ds(0, x_outer * (CORES - 1))], self.rn.at[c])

        def drain(self):
            take(self.act.at[:, pl.ds(0, x_outer - 1)], self.sf)
            take(self.act.at[:, pl.ds(0, x_outer * (CORES - 1))], self.sn)

        def rows(self, c, i):
            return self.act[c, :, i].reshape(total_t, piece)

    pre, back = Sums("pre", 2), Sums("back", 1)
    hidden_out, grad_out = Spread("act_h"), Spread("act_g")

    def mm_pre(c):
        for i, weight in enumerate((wg, wu)):
            pre.part[c, :, i] = dot(r["tok"][...], weight[c]).reshape(nx, tc, piece)
        pre.send(c)

    def mm_back(c):
        cot = all_cot[...].reshape(total_t, wide)
        back.part[c, :, 0] = dot_t(cot, wd[c]).reshape(nx, tc, piece)
        back.send(c)

    def act_hidden(c):
        pre.close(c)
        gate_pre = pre.full(c, 0) * gate_scale
        up_pre = pre.full(c, 1) * up_scale
        sig = jax.nn.sigmoid(gate_pre)
        hidden = (gate_pre * sig * up_pre).astype(BF16)
        hidden_out.act[c, gx, 0] = hidden
        hidden_out.send(c)
        r["slope"][c, 0] = up_pre * sig * (1.0 + gate_pre * (1.0 - sig))
        r["slope"][c, 1] = gate_pre * sig
        r["top_h"][...] = jnp.maximum(
            r["top_h"][...], fold(dot(hidden, r["tab_h"][...]))
        )

    def act_grad(c):
        back.close(c)
        grad = dot_wide(back.full(c, 0) * down_unit, r["tab_h"][...]) * hid_s
        for i in range(2):
            grad_out.act[c, gx, i] = (grad * r["slope"][c, i]).astype(BF16)
        grad_out.send(c)

    r["top_h"][...] = jnp.zeros((8, piece), F32)

    def when(cond, body, *args):
        @pl.when(cond)
        def _():
            body(*args)

    lead = 3
    inside = max(0, min(y_outer - 1, nc - lead))

    def cot_ready():
        for k in range(inside + 1, y_outer):
            g_forward(1, k)
        g_finish(1)

    start_y2, finish_y2 = exchange(
        ny, gy, "gy", r["tile2"], r["slots_y2"], r["q_y"]
    )
    start_x2, finish_x2 = exchange(
        nx, gx, "gx", r["mid2"], r["slots_x2"], r["q_x"]
    )

    def peak_one():
        r["tile2"][...] = peak_tile([jnp.max(r["top_h"][...]) * hid_s])
        start_y2()
        r["slots_y2"][0] = r["tile2"][...]

    def peak_two():
        finish_y2()
        r["mid2"][...] = jnp.max(r["slots_y2"][...], axis=0)
        start_x2()
        r["slots_x2"][0] = r["mid2"][...]

    def peak_three():
        loop(0, nc, hidden_out.arrive)
        finish_x2()
        top2 = jnp.max(r["slots_x2"][...], axis=0)
        r["mid3"][...] = top2
        hidden_inv = tile_scalar(1.0 / (top2 + tiny), 0) * hid_s

        def hidden_step(c):
            turned = dot(hidden_out.rows(c, 0), r["tab_h"][...])
            r["hid"][c] = soft(turned * hidden_inv)

        loop(0, nc, hidden_step)

    y_order = sorted(range(1, y_outer), key=lambda k: abs(2 * k - y_outer)) + [0]
    bufs = [r["out_part"], r["in_part"]]
    ones, twos, threes = r["y_one"], r["y_two"], r["y_three"]

    def y_near(i, k, o):
        j, to = lax.rem(y_hi + k, y_outer), lax.rem(y_lo + o, lanes)
        return remote(
            bufs[i].at[lanes * j + to], ones.at[i, k, o - 1], r["y_s1"].at[i],
            r["y_r1"].at[i, k], {"gy": lanes * y_hi + to},
        )

    def y_far(i, k):
        j = lax.rem(y_hi + k, y_outer)
        return remote(
            twos.at[i, k - 1], threes.at[i, k - 1], r["y_s2"].at[i],
            r["y_r2"].at[i], {"gy": lanes * j + y_lo},
        )

    def y_send(i):
        for k in y_order:
            for o in range(1, lanes):
                y_near(i, k, o).start()

    def y_sum(i, k):
        total = bufs[i][lanes * lax.rem(y_hi + k, y_outer) + y_lo].astype(F32)
        for o in range(1, lanes):
            total = total + ones[i, k, o - 1].astype(F32)
        return total

    def y_pass(i, k):
        take(ones.at[i, k], r["y_r1"].at[i, k])
        twos[i, k - 1] = y_sum(i, k).astype(BF16)
        y_far(i, k).start()

    def y_close(i):
        take(ones.at[i, 0], r["y_r1"].at[i, 0])
        total = y_sum(i, 0)
        take(threes.at[i], r["y_r2"].at[i])
        for k in y_order[:-1]:
            total = total + threes[i, k - 1].astype(F32)
        return total

    def out_step(b):
        cols = ds(b, band)
        total = jnp.zeros((total_t, band), F32)
        for c in range(nc):
            total = total + dot(r["hid"][c], wd[c, :, cols])
        r["out_part"][:, :, cols] = total.astype(BF16).reshape(ny, tl, band)

    def out_all():
        loop(0, nb, out_step)
        y_send(0)

    def out_pass():
        for k in y_order[:-1]:
            y_pass(0, k)

    def y_drain(i):
        take(ones.at[i], r["y_s1"].at[i])
        take(threes.at[i], r["y_s2"].at[i])

    def in_sum(c, rows):
        gate_sum = dot_t(grad_out.rows(c, 0), wg[c, rows, :]) * gate_unit
        return gate_sum + dot_t(grad_out.rows(c, 1), wu[c, rows, :]) * up_unit

    def in_step(c):
        grad_out.arrive(c)
        for b in range(nb):
            rows = slice(b * band, (b + 1) * band)
            r["acc"][:, rows] += in_sum(c, rows)

    def in_last():
        grad_out.arrive(nc - 1)
        for b in range(nb):
            rows = slice(b * band, (b + 1) * band)
            total = r["acc"][:, rows] + in_sum(nc - 1, rows)
            r["in_part"][:, :, rows] = total.astype(BF16).reshape(ny, tl, band)
        y_send(1)

    r["acc"][...] = jnp.zeros((total_t, wide), F32)

    def turn_tokens():
        for b in range(nb):
            cols = slice(b * band, (b + 1) * band)
            turned = dot(r["tok"][:, cols], r["tab_w"][...]) * tok_s
            r["tok_t"][cols, :] = turned.T.astype(BF16)

    def pipe(i):
        def both(lag, one, two):
            when((i >= lag) & (i < nc + lag), one, i - lag)
            when((i >= nc + lag) & (i < 2 * nc + lag), two, i - nc - lag)

        both(0, pre.turn, back.turn)
        if inside:
            when((i >= lead) & (i < lead + inside), g_forward, 1, i - lead + 1)
        when(i == nc - 1, cot_ready)
        both(-1, mm_pre, mm_back)
        both(LAG, act_hidden, act_grad)
        when(i == nc - 1 + LAG, peak_one)
        both(2 * LAG, hidden_out.forward, grad_out.forward)
        both(-2, cast_gate_up, cast_down)
        when(i == nc + 1 + LAG, peak_two)
        first_in = nc + 2 * LAG + 1
        when((i >= first_in) & (i < first_in + nc - 1), in_step, i - first_in)
        when(i == nc + 2 * LAG + 1, peak_three)
        when(i == nc + 2 * LAG + 2, out_all)
        when(i == nc + 2 * LAG + 3, turn_tokens)
        when(i == nc + 2 * LAG + 4, out_pass)

    cast_gate_up(0)
    mm_pre(0)
    (cast_gate_up(1) if nc > 1 else cast_down(0))
    loop(0, max(2 * nc + 2 * LAG, nc + 2 * LAG + 5), pipe)
    in_last()

    top2 = r["mid3"][...]
    hidden_unit = tile_scalar(top2 / fp_top, 0)
    out_scale = tile_scalar(top2[0:1, :] * top[3:4, :] / (fp_top * fp_top), 0)

    def gate_up_grads(c):
        for b in range(nb):
            rows = slice(b * band, (b + 1) * band)
            for i, weight in enumerate((wg, wu)):
                weight[c, rows, :] = (
                    dot(r["tok_t"][rows, :], grad_out.rows(c, i)) * tok_unit
                ).astype(BF16)

    def down_grads(c):
        turned = (dot(r["hid"][c], r["tab_h"][...]) * hid_s).T.astype(BF16)
        cot = all_cot[...].reshape(total_t, wide)
        wd[c] = (dot(turned, cot) * hidden_unit).astype(BF16)

    loop(0, nc, gate_up_grads)
    cuts = [nc * k // y_outer for k in range(y_outer + 1)]
    for n, k in enumerate(y_order):
        if k:
            y_pass(1, k)
        loop(cuts[n], cuts[n + 1], down_grads)
    r["output"][...] = (y_close(0) * out_scale).astype(BF16)
    pre.drain()
    back.drain()
    hidden_out.drain()
    grad_out.drain()
    for i in range(2):
        g_drain(i)
        y_drain(i)
    total = y_close(1)
    for b in range(nb):
        cols = slice(b * band, (b + 1) * band)
        r["input_grad"][:, cols] = (
            dot_wide(total[:, cols], r["tab_w"][...]) * tok_s
        ).astype(BF16)


def store_kernel(nc, piece, *refs):
    small, grads, outs, sems = refs[:2], refs[2:5], refs[5:10], refs[10]
    copies = [
        pltpu.make_async_copy(small[i], outs[i], sems.at[i, 0]) for i in range(2)
    ]
    for c in range(nc):
        cols = pl.ds(c * piece, piece)
        for i in range(3):
            dst = outs[2 + i].at[cols, :] if i == 2 else outs[2 + i].at[:, cols]
            copies.append(pltpu.make_async_copy(grads[i].at[c], dst, sems.at[2 + i, c]))
    for copy in copies:
        copy.start()
    for copy in copies:
        copy.wait()


def shards(nx, ny, tokens, cotangent, gate_weight, up_weight, down_weight):
    lanes = 1 << max((ny.bit_length() - 2) // 2, 0)
    tl, wide = tokens.shape
    hid = gate_weight.shape[1]
    piece = 256 if hid % 256 == 0 else hid
    band = 256 if wide % 256 == 0 else wide
    nc = hid // piece
    total_t = tl * ny
    tc = total_t // nx
    x_outer, y_outer = nx // CORES, ny // lanes
    dims = (nx, ny, lanes, tl, wide, hid, piece, band)
    ins = ["tokens", "cot", "gate", "up", "down"]
    outs = ["output", "input_grad", "wg", "wu", "wd"]
    tile = pltpu.VMEM((8, 128), F32)
    scratch = {
        "load": DMA((3, nc)), "own": DMA((2,)),
        "all_tok": pltpu.VMEM((ny, tl, wide), BF16),
        "all_cot": pltpu.VMEM((ny, tl, wide), BF16),
        "g_sf": DMA((2,)), "g_rf": DMA((2, y_outer - 1)),
        "g_sn": DMA((2,)), "g_rn": DMA((2,)),
        "tab_w": pltpu.VMEM((band, band), BF16),
        "tab_h": pltpu.VMEM((piece, piece), BF16),
        "tile": tile, "mid": tile, "tile2": tile, "mid2": tile, "mid3": tile,
        "slots_x": pltpu.VMEM((nx, 8, 128), F32),
        "slots_y": pltpu.VMEM((ny, 8, 128), F32),
        "slots_x2": pltpu.VMEM((nx, 8, 128), F32),
        "slots_y2": pltpu.VMEM((ny, 8, 128), F32),
        "p_x": DMA((2,)), "p_y": DMA((2,)), "q_x": DMA((2,)), "q_y": DMA((2,)),
        "tok": pltpu.VMEM((total_t, wide), BF16),
        "tok_t": pltpu.VMEM((wide, total_t), BF16),
        "slope": pltpu.VMEM((nc, 2, tc, piece), F32),
        "hid": pltpu.VMEM((nc, total_t, piece), BF16),
        "acc": pltpu.VMEM((total_t, wide), F32),
        "top_h": pltpu.VMEM((8, piece), F32),
        "out_part": pltpu.VMEM((ny, tl, wide), BF16),
        "in_part": pltpu.VMEM((ny, tl, wide), BF16),
        "y_one": pltpu.VMEM((2, y_outer, lanes - 1, tl, wide), BF16),
        "y_two": pltpu.VMEM((2, y_outer - 1, tl, wide), BF16),
        "y_three": pltpu.VMEM((2, y_outer - 1, tl, wide), BF16),
        "y_s1": DMA((2,)), "y_r1": DMA((2, y_outer)),
        "y_s2": DMA((2,)), "y_r2": DMA((2,)),
    }
    for tag, count in (("pre", 2), ("back", 1)):
        block = (count, tc, piece)
        scratch[tag + "_part"] = pltpu.VMEM((nc, nx) + block, F32)
        scratch[tag + "_first"] = pltpu.VMEM((nc, x_outer, CORES - 1) + block, F32)
        scratch[tag + "_second"] = pltpu.VMEM((nc, x_outer - 1) + block, BF16)
        scratch[tag + "_third"] = pltpu.VMEM((nc, x_outer - 1) + block, BF16)
        scratch[tag + "_s"] = DMA((2,))
        scratch[tag + "_r1"] = DMA((nc, x_outer))
        scratch[tag + "_r2"] = DMA((nc, x_outer - 1))
    for tag, count in (("act_h", 1), ("act_g", 2)):
        scratch[tag] = pltpu.VMEM((nc, nx, count, tc, piece), BF16)
        scratch[tag + "_s"] = DMA((2,))
        scratch[tag + "_rf"] = DMA((nc, x_outer - 1))
        scratch[tag + "_rn"] = DMA((nc,))
    names = tuple(ins + outs + list(scratch))
    small = jax.ShapeDtypeStruct(tokens.shape, BF16)
    small_vmem = pltpu.VMEM(tokens.shape, BF16)
    columns = pltpu.VMEM((nc, wide, piece), BF16)
    rows = pltpu.VMEM((nc, piece, wide), BF16)
    results = pl.pallas_call(
        functools.partial(layer_kernel, dims, names),
        out_shape=[small_vmem, small_vmem, columns, columns, rows],
        in_specs=[HBM] * 5,
        out_specs=[VMEM] * 5,
        scratch_shapes=list(scratch.values()),
        compiler_params=pltpu.CompilerParams(
            collective_id=0, has_side_effects=True, vmem_limit_bytes=VMEM_MIB * 2 ** 20
        ),
    )(tokens, cotangent, gate_weight, up_weight, down_weight)
    return pl.pallas_call(
        functools.partial(store_kernel, nc, piece),
        out_shape=[small, small] + [
            jax.ShapeDtypeStruct(w.shape, BF16)
            for w in (gate_weight, up_weight, down_weight)
        ],
        in_specs=[VMEM] * 5,
        out_specs=[HBM] * 5,
        scratch_shapes=[DMA((5, nc))],
        compiler_params=pltpu.CompilerParams(vmem_limit_bytes=STORE_MIB * 2 ** 20),
    )(*results)


def solution(mesh):
    in_specs = (P("gy", "gx"), P("gy", "gx"), P("gx", "gy"), P("gx", "gy"), P("gy", "gx"))
    out_specs = (P("gy", "gx"), P("gy", "gx"), P("gx", "gy"), P("gx", "gy"), P("gy", "gx"))
    nx, ny = mesh.shape["gx"], mesh.shape["gy"]
    return jax.shard_map(
        functools.partial(shards, nx, ny),
        mesh=mesh, in_specs=in_specs, out_specs=out_specs, check_vma=False,
    )
```

time: 100 us -> 73.6 us (0.74)
  Pallas kernels: 86.8 us -> 72.8 us
  local copies, waits for them, and re-layouts: 12.4 us -> 0 us
    pallas_call x1, Pallas kernels: 86.8 us -> 68.4 us  [shards(): pl.pallas_call(functools.partial(layer_kernel, dims, names), out_shape=[s...]
    unnamed x9 -> x0, local copies, waits for them, and re-layouts: 12.4 us -> none
    pallas_call x0 -> x1, Pallas kernels: none -> 4.42 us  [shards(): pl.pallas_call(functools.partial(store_kernel, nc, piece), out_shape=[sma...]
where the time goes in v2:
time: 73.6 us; the launch traced here: 73.5 us
  Pallas kernels  72.8 us (99%)
    pallas_call x1, Pallas kernels, shards(): pl.pallas_call(functools.partial(layer_kernel, dims, names), out_shape=[s...  68.4 us
    pallas_call x1, Pallas kernels, shards(): pl.pallas_call(functools.partial(store_kernel, nc, piece), out_shape=[sma...  4.42 us

profile of v2, /device:TPU:0, one launch (start us, length us, event | category | flops | bytes accessed | tf_op | source)
XLA Modules:
  0.0 73.5 jit_solution(2889769301573065097)
XLA Ops:
  0.6 68.4 %shard_map.92 = (bf16[32,1024]{1,0:T(8,128)(2,1)S(1)}, bf16[32,1024]{1,0:T(8,128)(2,1)S(1)}, bf16[7,1024,256]{2,1,0:T(8,128)(2,1)S(1)}, bf16[7,1024,256]{2,1,0:T(8,128)(2,1)S(1)}, bf16[7,256,1024]{2,1,0:T(8,128)(2,1)S(1)}) custom-call(bf16[32,1024]{1,0:T(8,128)(2,1)} %refs_0_.1, bf16[32,1024]{1,0:T(8,128)(2,1)} %refs_1_.1, bf16[1024,1792]{1,0:T(8,128)(2,1)} %refs_2_.1, ...), custom_call_target="tpu_custom_call" | custom-call | tf_op jit(solution)/shard_map/pallas_call | solution.py:680
  69.1 4.4 %shard_map.93 = (bf16[32,1024]{1,0:T(8,128)(2,1)}, bf16[32,1024]{1,0:T(8,128)(2,1)}, bf16[1024,1792]{1,0:T(8,128)(2,1)}, bf16[1024,1792]{1,0:T(8,128)(2,1)}, bf16[1792,1024]{1,0:T(8,128)(2,1)}) custom-call(bf16[32,1024]{1,0:T(8,128)(2,1)S(1)} %get-tuple-element.10.refs_0_, bf16[32,1024]{1,0:T(8,128)(2,1)S(1)} %get-tuple-element.11.refs_1_, ...), custom_call_target="tpu_custom_call" | custom-call | tf_op jit(solution)/shard_map/pallas_call | solution.py:690

commit v3 on v2

v3 whole, which is shorter than its diff:
```python
import functools

import jax
import jax.numpy as jnp
from jax import lax
from jax.experimental import pallas as pl
from jax.experimental.pallas import tpu as pltpu
from jax.sharding import PartitionSpec as P

ROT_BLOCK = 128
HID_BLOCK = 64
CORES = 2
VMEM_MIB = 50
STORE_MIB = 12
LAG = 2
SPLIT = 1

fp_top = 448.0
tiny = 1e-06

MESH = pl.DeviceIdType.MESH
VMEM = pl.BlockSpec(memory_space=pltpu.VMEM)
HBM = pl.BlockSpec(memory_space=pltpu.HBM)
DMA = pltpu.SemaphoreType.DMA
F32 = jnp.float32
BF16 = jnp.bfloat16


def rot_table(size, block):
    shift = block.bit_length() - 1
    row = lax.broadcasted_iota(jnp.int32, (size, size), 0)
    col = lax.broadcasted_iota(jnp.int32, (size, size), 1)
    bits = row & col & (block - 1)
    bits = bits ^ (bits >> 4)
    bits = bits ^ (bits >> 2)
    bits = bits ^ (bits >> 1)
    sign = 1 - 2 * (bits & 1)
    return jnp.where((row >> shift) == (col >> shift), sign, 0).astype(F32).astype(BF16)


def dot(left, right):
    return jnp.dot(left, right, preferred_element_type=F32)


def dot_t(left, right):
    return lax.dot_general(
        left, right, (((1,), (1,)), ((), ())), preferred_element_type=F32
    )


def dot_wide(values, table):
    high = values.astype(BF16)
    rest = values - high.astype(F32)
    mid = rest.astype(BF16)
    low = (rest - mid.astype(F32)).astype(BF16)
    return dot(high, table) + (dot(mid, table) + dot(low, table))


def remote(src, dst, send, recv, target):
    return pltpu.make_async_remote_copy(
        src_ref=src, dst_ref=dst, send_sem=send, recv_sem=recv,
        device_id=target, device_id_type=MESH,
    )


def loop(low, high, body):
    def step(i, carry):
        body(i)
        return carry
    lax.fori_loop(low, high, step, 0)


def greet(nx, ny, gx, gy):
    barrier = pltpu.get_barrier_semaphore()
    for n, me, axis in ((nx, gx, "gx"), (ny, gy, "gy")):

        def hello(k, n=n, me=me, axis=axis):
            pl.semaphore_signal(
                barrier, inc=1, device_id={axis: lax.rem(me + k, n)}, device_id_type=MESH
            )

        loop(1, n, hello)
    return lambda: pl.semaphore_wait(barrier, nx - 1 + ny - 1)


def take(ref, sem):
    pltpu.make_async_copy(ref, ref, sem).wait()


def share_peaks(n, me, axis, slots, sems):
    def start(k):
        target = {axis: lax.rem(me + k, n)}
        remote(slots.at[0], slots.at[k], sems.at[0], sems.at[1], target).start()

    def finish():
        rest = slots.at[pl.ds(1, n - 1)]
        take(rest, sems.at[0])
        take(rest, sems.at[1])
        return jnp.max(slots[...], axis=0)

    return (lambda: loop(1, n, start)), finish


def fold(values):
    rows, cols = values.shape
    return jnp.max(jnp.abs(values).reshape(rows // 8, 8, cols), axis=0)


def ds(i, size):
    return pl.ds(pl.multiple_of(i * size, size), size)


def lane_ids():
    return lax.broadcasted_iota(jnp.int32, (1, 128), 1)


def peak_row(values):
    row = jnp.zeros((1, 128), F32)
    for i, value in enumerate(values):
        row = jnp.where(lane_ids() == i, value, row)
    return row


def lane_scalar(row, i):
    return jnp.max(jnp.where(lane_ids() == i, row, 0.0))


def layer_kernel(dims, names, *refs):
    nx, ny, lanes, tl, wide, hid, piece, band = dims
    r = dict(zip(names, refs))
    total_t = tl * ny
    hl, th = tl // 2, total_t // nx // 2
    nc = hid // piece
    nb = wide // band
    tail = min(SPLIT, nc)
    gx, gy = lax.axis_index("gx"), lax.axis_index("gy")
    tok_s, hid_s = ROT_BLOCK ** (-0.5), HID_BLOCK ** (-0.5)
    wg, wu, wd = r["wg"], r["wu"], r["wd"]
    all_tok, all_cot = r["all_tok"], r["all_cot"]

    def own_load(i, h):
        src, dst = ((r["tokens"], all_tok), (r["cot"], all_cot))[i]
        src = src.at[pl.ds(h * hl, hl)]
        return pltpu.make_async_copy(src, dst.at[h, gy], r["own"].at[i, h])

    own_load(0, 0).start()
    own_load(0, 1).start()
    greeted = greet(nx, ny, gx, gy)
    own_load(1, 0).start()
    own_load(1, 1).start()

    def load(i, c):
        cols = ds(c, piece)
        src, dst = [
            (r["gate"].at[:, cols], wg.at[c]),
            (r["up"].at[:, cols], wu.at[c]),
            (r["down"].at[cols, :], wd.at[c]),
        ][i]
        return pltpu.make_async_copy(src, dst, r["load"].at[i, c])

    def start_loads(c):
        for i in range(3):
            load(i, c).start()

    loop(0, nc, start_loads)
    r["tab_w"][...] = rot_table(band, ROT_BLOCK)
    r["tab_h"][...] = rot_table(piece, HID_BLOCK)
    own_load(0, 0).wait()
    own_load(0, 1).wait()
    tok_top = jnp.zeros((8, band), F32)
    for b in range(nb):
        cols = slice(b * band, (b + 1) * band)
        tok_top = jnp.maximum(tok_top, fold(dot(all_tok[:, gy, :, cols].reshape(tl, band), r["tab_w"][...])))

    def peak_step(c, tops):
        gate_top, up_top, down_top = tops
        for i in range(3):
            load(i, c).wait()
        for b in range(nb):
            rows = slice(b * band, (b + 1) * band)
            gate_top = jnp.maximum(gate_top, fold(dot(r["tab_w"][...], wg[c, rows, :])))
            up_top = jnp.maximum(up_top, fold(dot(r["tab_w"][...], wu[c, rows, :])))
            down_top = jnp.maximum(down_top, fold(dot(r["tab_h"][...], wd[c, :, rows])))
        return gate_top, up_top, down_top

    tops = (
        jnp.zeros((8, piece), F32), jnp.zeros((8, piece), F32), jnp.zeros((8, band), F32)
    )
    early = nc // 2
    tops = lax.fori_loop(0, early, peak_step, tops)
    greeted()

    y_outer = ny // lanes
    y_hi, y_lo = gy // lanes, lax.rem(gy, lanes)
    g_all = [all_tok, all_cot]

    relay = wide // 4
    cuts = pl.ds(0, wide - relay), pl.ds(wide - relay, relay)

    def g_far(i, p, k, slot):
        j = lax.rem(y_hi + k, y_outer)
        ref = g_all[i].at[:, slot, :, cuts[p]]
        recv = r["g_rf"].at[i, 0 if p else k]
        return remote(ref, ref, r["g_sf"].at[i, p], recv, {"gy": lanes * j + y_lo})

    def g_near(i, o, ref, recv):
        target = {"gy": lanes * y_hi + lax.rem(y_lo + o, lanes)}
        return remote(ref, ref, recv[0], recv[1], target)

    y_mid = sorted(range(1, y_outer), key=lambda k: abs(2 * k - y_outer))
    flip = 2 * y_hi // y_outer
    side = y_hi + flip * (y_outer - 1 - 2 * y_hi)

    def far_first(n):
        back = y_outer - 2 - y_hi + flip + (2 * flip - 1) * n
        return lax.rem(back + 2 * (y_outer - 1), y_outer - 1) + 1

    def near_first(n):
        paired = n < 2 * side
        step = jnp.where(paired, n // 2 + 1, n - side + 1)
        down = jnp.where(paired, 1 - 2 * (n % 2), -1) * (1 - 2 * flip)
        return lax.rem(down * step + y_outer, y_outer)

    def g_start(i):
        for o in range(1, lanes):
            g_near(i, o, g_all[i].at[:, gy], (r["g_sn"].at[i, 0], r["g_rn"].at[i, 0])).start()
        for n in range(y_outer - 1):
            g_far(i, 0, far_first(n), gy).start()

    def g_relay(i):
        for n in range(y_outer - 1):
            g_far(i, 1, far_first(n), gy).start()
        take(g_all[i].at[:, pl.ds(0, lanes - 1)], r["g_rn"].at[i, 0])
        for o in range(1, lanes):
            beside = lanes * y_hi + lax.rem(y_lo + o, lanes)
            for n in range(y_outer - 1):
                g_far(i, 1, far_first(n), beside).start()

    def g_forward(i, k):
        mine = lanes * lax.rem(y_hi + y_outer - k, y_outer) + y_lo
        g_far(i, 0, k, mine).wait_recv()
        ref = g_all[i].at[:, mine, :, cuts[0]]
        for o in range(1, lanes):
            g_near(i, o, ref, (r["g_sn"].at[i, 1], r["g_rn"].at[i, 1])).start()

    def g_blocks(i, p, count):
        return g_all[i].at[:, pl.ds(0, count), :, cuts[p]]

    def g_finish(i):
        take(g_blocks(i, 0, (y_outer - 1) * (lanes - 1)), r["g_rn"].at[i, 1])
        take(g_blocks(i, 1, (y_outer - 1) * lanes), r["g_rf"].at[i, 0])

    def g_drain(i):
        take(g_all[i].at[:, pl.ds(0, lanes - 1)], r["g_sn"].at[i, 0])
        take(g_blocks(i, 0, (y_outer - 1) * (lanes - 1)), r["g_sn"].at[i, 1])
        take(g_blocks(i, 0, y_outer - 1), r["g_sf"].at[i, 0])
        take(g_blocks(i, 1, (y_outer - 1) * lanes), r["g_sf"].at[i, 1])

    g_start(0)

    tops = lax.fori_loop(early, nc, peak_step, tops)
    start_x, finish_x = share_peaks(nx, gx, "gx", r["slots_x"], r["p_x"])
    start_y, finish_y = share_peaks(ny, gy, "gy", r["slots_y"], r["p_y"])
    r["slots_x"][0] = peak_row([
        jnp.max(tok_top) * tok_s, jnp.max(tops[0]) * tok_s,
        jnp.max(tops[1]) * tok_s, jnp.max(tops[2]) * hid_s,
    ])
    start_x()
    g_relay(0)
    g_forward(0, near_first(0))
    r["slots_y"][0] = finish_x()
    start_y()
    for n in range(1, y_outer - 1):
        g_forward(0, near_first(n))
    top = finish_y()
    own_load(1, 0).wait()
    own_load(1, 1).wait()
    g_start(1)
    inverse = 1.0 / (top + tiny)
    unit = top / fp_top
    pair = lane_scalar(top, 0) * top / (fp_top * fp_top)
    tok_inv = lane_scalar(inverse, 0) * tok_s
    gate_inv = lane_scalar(inverse, 1) * tok_s
    up_inv = lane_scalar(inverse, 2) * tok_s
    down_inv = lane_scalar(inverse, 3) * hid_s
    tok_unit, gate_unit, up_unit, down_unit = (lane_scalar(unit, i) for i in range(4))
    gate_scale, up_scale = lane_scalar(pair, 1), lane_scalar(pair, 2)

    def soft(values):
        return (fp_top * jnp.tanh(values)).astype(BF16)

    def cast_gate_up(c):
        for b in range(nb):
            rows = slice(b * band, (b + 1) * band)
            wg[c, rows, :] = soft(dot(r["tab_w"][...], wg[c, rows, :]) * gate_inv)
            wu[c, rows, :] = soft(dot(r["tab_w"][...], wu[c, rows, :]) * up_inv)

    def cast_down(c):
        for b in range(nb):
            rows = slice(b * band, (b + 1) * band)
            wd[c, :, rows] = soft(dot(r["tab_h"][...], wd[c, :, rows]) * down_inv)

    x_outer = nx // CORES
    x_hi, x_lo = gx // CORES, lax.rem(gx, CORES)
    x_order = list(range(1, x_outer)) + [0]

    def span(h):
        return pl.ds(0, 2) if h is None else pl.ds(h, 1)

    def order(c, h):
        return c + tail if h == 1 else c

    class Sums:
        def __init__(self, tag, count):
            self.count = count
            self.part, self.first = r[tag + "_part"], r[tag + "_first"]
            self.second, self.third = r[tag + "_second"], r[tag + "_third"]
            self.s1, self.r1 = r[tag + "_s"].at[0], r[tag + "_r1"]
            self.s2, self.r2 = r[tag + "_s"].at[1], r[tag + "_r2"]

        def far(self, c, h, k):
            j = lax.rem(x_hi + k, x_outer)
            return remote(
                self.second.at[c, k - 1, span(h)], self.third.at[c, k - 1, span(h)],
                self.s2, self.r2.at[order(c, h), k - 1], {"gx": CORES * j + x_lo},
            )

        def send(self, c, h):
            for k in x_order:
                j = lax.rem(x_hi + k, x_outer)
                for o in range(1, CORES):
                    to = lax.rem(x_lo + o, CORES)
                    remote(
                        self.part.at[c, span(h), CORES * j + to],
                        self.first.at[c, k, o - 1, span(h)],
                        self.s1, self.r1.at[order(c, h)], {"gx": CORES * x_hi + to},
                    ).start()

        def near_sum(self, c, h, k, i):
            slot = CORES * lax.rem(x_hi + k, x_outer) + x_lo
            total = self.part[c, span(h), slot, i]
            for o in range(1, CORES):
                total = total + self.first[c, k, o - 1, span(h), i]
            return total

        def turn(self, c, h):
            whole = self.first.at[c, pl.ds(0, x_outer), pl.ds(0, CORES - 1), span(h)]
            take(whole, self.r1.at[order(c, h)])
            for k in x_order[:-1]:
                for i in range(self.count):
                    self.second[c, k - 1, span(h), i] = self.near_sum(c, h, k, i).astype(
                        BF16
                    )
                self.far(c, h, k).start()

        def close(self, c, h):
            for k in x_order[:-1]:
                self.far(c, h, k).wait_recv()

        def drain(self):
            take(self.first, self.s1)
            take(self.third, self.s2)

        def full(self, c, h, i):
            total = self.near_sum(c, h, 0, i)
            for k in x_order[:-1]:
                total = total + self.third[c, k - 1, span(h), i].astype(F32)
            return total.reshape(-1, piece)

    class Spread:
        def __init__(self, tag):
            self.act = r[tag]
            self.sf, self.rf = r[tag + "_s"].at[0], r[tag + "_rf"]
            self.sn, self.rn = r[tag + "_s"].at[1], r[tag + "_rn"]

        def far(self, c, h, k, slot):
            ref = self.act.at[c, span(h), slot]
            target = {"gx": CORES * lax.rem(x_hi + k, x_outer) + x_lo}
            return remote(ref, ref, self.sf, self.rf.at[order(c, h), k - 1], target)

        def near(self, c, h, o, slot):
            ref = self.act.at[c, span(h), slot]
            target = {"gx": CORES * x_hi + lax.rem(x_lo + o, CORES)}
            return remote(ref, ref, self.sn, self.rn.at[order(c, h)], target)

        def put(self, c, h, i, values):
            self.act[c, span(h), gx, i] = values.astype(BF16).reshape(-1, th, piece)

        def send(self, c, h):
            for k in range(1, x_outer):
                self.far(c, h, k, gx).start()
            for o in range(1, CORES):
                self.near(c, h, o, gx).start()

        def forward(self, c, h):
            for k in range(1, x_outer):
                mine = CORES * lax.rem(x_hi + x_outer - k, x_outer) + x_lo
                self.far(c, h, k, mine).wait_recv()
                for o in range(1, CORES):
                    self.near(c, h, o, mine).start()

        def arrive(self, c, h=None):
            some = pl.ds(0, x_outer * (CORES - 1))
            take(self.act.at[c, span(h), some], self.rn.at[order(c, h)])

        def drain(self):
            take(self.act.at[:, :, pl.ds(0, x_outer - 1)], self.sf)
            take(self.act.at[:, :, pl.ds(0, x_outer * (CORES - 1))], self.sn)

        def rows(self, c, i, h=None):
            return self.act[c, span(h), :, i].reshape(-1, piece)

    pre, back = Sums("pre", 2), Sums("back", 1)
    hidden_out, grad_out = Spread("act_h"), Spread("act_g")

    def mm_pre(c, h):
        for i, weight in enumerate((wg, wu)):
            total = dot(r["tok"][...], weight[c])
            pre.part[c, :, :, i] = total.reshape(2, nx, th, piece)
        pre.send(c, h)

    def mm_back(c, h):
        cot = all_cot[span(h)].reshape(-1, wide)
        back.part[c, span(h), :, 0] = dot_t(cot, wd[c]).reshape(-1, nx, th, piece)
        back.send(c, h)

    def act_hidden(c, h):
        pre.close(c, h)
        gate_pre = pre.full(c, h, 0) * gate_scale
        up_pre = pre.full(c, h, 1) * up_scale
        sig = jax.nn.sigmoid(gate_pre)
        hidden = (gate_pre * sig * up_pre).astype(BF16)
        hidden_out.put(c, h, 0, hidden)
        hidden_out.send(c, h)
        slope = up_pre * sig * (1.0 + gate_pre * (1.0 - sig))
        r["slope"][c, 0] = slope.reshape(2, th, piece)
        r["slope"][c, 1] = (gate_pre * sig).reshape(2, th, piece)
        r["top_h"][...] = jnp.maximum(
            r["top_h"][...], fold(dot(hidden, r["tab_h"][...]))
        )

    def act_grad(c, h):
        back.close(c, h)
        grad = dot_wide(back.full(c, h, 0) * down_unit, r["tab_h"][...]) * hid_s
        for i in range(2):
            slope = r["slope"][c, i, span(h)].reshape(-1, piece)
            grad_out.put(c, h, i, grad * slope)
        grad_out.send(c, h)

    r["top_h"][...] = jnp.zeros((8, piece), F32)

    def when(cond, body, *args):
        @pl.when(cond)
        def _():
            body(*args)

    lead = 3
    inside = max(0, min(y_outer - 1, nc - lead))

    def forward_cot(n):
        when(n == 0, g_relay, 1)
        g_forward(1, near_first(n))

    def cot_ready():
        if not inside:
            g_relay(1)
        for n in range(inside, y_outer - 1):
            g_forward(1, near_first(n))
        g_finish(1)

    start_y2, finish_y2 = share_peaks(ny, gy, "gy", r["slots_y2"], r["q_y"])
    start_x2, finish_x2 = share_peaks(nx, gx, "gx", r["slots_x2"], r["q_x"])

    def peak_one():
        r["slots_y2"][0] = peak_row([jnp.max(r["top_h"][...]) * hid_s])
        start_y2()

    def peak_two():
        r["slots_x2"][0] = finish_y2()
        start_x2()

    def peak_three():
        loop(0, nc, hidden_out.arrive)
        top2 = finish_x2()
        r["mid"][...] = top2
        hidden_inv = lane_scalar(1.0 / (top2 + tiny), 0) * hid_s

        def hidden_step(c):
            turned = dot(hidden_out.rows(c, 0), r["tab_h"][...])
            r["hid"][c] = soft(turned * hidden_inv)

        loop(0, nc, hidden_step)

    y_order = y_mid + [0]
    def y_block(i, d):
        return r["in_part"].at[i - 1, d] if i else r["out_part"].at[:, d]

    def y_refs(name):
        return [r[name + "_o"]] + [r[name + "_i"].at[p] for p in range(2)]

    ones, twos, threes = (y_refs(name) for name in ("y_one", "y_two", "y_three"))

    def y_near(i, k, o):
        j, to = lax.rem(y_hi + k, y_outer), lax.rem(y_lo + o, lanes)
        return remote(
            y_block(i, lanes * j + to), ones[i].at[k, o - 1], r["y_s1"].at[i],
            r["y_r1"].at[i, k], {"gy": lanes * y_hi + to},
        )

    def y_far(i, k):
        j = lax.rem(y_hi + k, y_outer)
        return remote(
            twos[i].at[k - 1], threes[i].at[k - 1], r["y_s2"].at[i],
            r["y_r2"].at[i], {"gy": lanes * j + y_lo},
        )

    def y_send(i):
        for k in y_order:
            for o in range(1, lanes):
                y_near(i, k, o).start()

    def y_sum(i, k):
        total = y_block(i, lanes * lax.rem(y_hi + k, y_outer) + y_lo)[...].astype(F32)
        for o in range(1, lanes):
            total = total + ones[i][k, o - 1].astype(F32)
        return total

    def y_pass(i, k):
        take(ones[i].at[k], r["y_r1"].at[i, k])
        twos[i][k - 1] = y_sum(i, k).astype(BF16)
        y_far(i, k).start()

    def y_close(i):
        take(ones[i].at[0], r["y_r1"].at[i, 0])
        total = y_sum(i, 0)
        take(threes[i], r["y_r2"].at[i])
        for k in y_order[:-1]:
            total = total + threes[i][k - 1].astype(F32)
        return total

    def out_step(b):
        cols = ds(b, band)
        total = jnp.zeros((total_t, band), F32)
        for c in range(nc):
            total = total + dot(r["hid"][c], wd[c, :, cols])
        r["out_part"][:, :, :, cols] = total.astype(BF16).reshape(2, ny, hl, band)

    def out_all():
        loop(0, nb, out_step)
        y_send(0)

    def y_drain(i):
        take(ones[i], r["y_s1"].at[i])
        take(threes[i], r["y_s2"].at[i])

    def in_sum(c, h, rows):
        gate_sum = dot_t(grad_out.rows(c, 0, h), wg[c, rows, :]) * gate_unit
        total = gate_sum + dot_t(grad_out.rows(c, 1, h), wu[c, rows, :]) * up_unit
        return total.reshape(-1, total_t // 2, band)

    def in_step(c, h):
        grad_out.arrive(c, h)
        for b in range(nb):
            rows = slice(b * band, (b + 1) * band)
            r["acc"][span(h), :, rows] += in_sum(c, h, rows)

    def in_last(h):
        grad_out.arrive(nc - 1, h)
        for b in range(nb):
            rows = slice(b * band, (b + 1) * band)
            total = r["acc"][span(h), :, rows] + in_sum(nc - 1, h, rows)
            r["in_part"][h, :, :, rows] = total.astype(BF16).reshape(ny, hl, band)
        y_send(1 + h)

    r["acc"][...] = jnp.zeros((2, total_t // 2, wide), F32)

    def down_grads(low, high):
        hidden_unit = lane_scalar(r["mid"][...] / fp_top, 0)

        def one(c):
            turned = (dot(r["hid"][c], r["tab_h"][...]) * hid_s).T.astype(BF16)
            cot = all_cot[...].reshape(total_t, wide)
            wd[c] = (dot(turned, cot) * hidden_unit).astype(BF16)

        loop(low, high, one)

    def turn_tokens():
        for b in range(nb):
            cols = slice(b * band, (b + 1) * band)
            turned = dot(r["tok"][:, cols], r["tab_w"][...]) * tok_s
            r["tok_t"][cols, :] = turned.T.astype(BF16)

    head = nc - tail
    parts = [(0, head, None), (head, tail, 0), (head + tail, tail, 1)]

    def pipe(i):
        def back_items(first, body):
            for low, count, h in parts:
                if count:
                    at = first + low
                    c = i - at + (0 if h is None else head)
                    when((i >= at) & (i < at + count), body, c, h)

        def both(lag, one, two):
            when((i >= lag) & (i < nc + lag), one, i - lag, None)
            back_items(nc + lag, two)

        both(0, pre.turn, back.turn)
        if inside:
            when((i >= lead) & (i < lead + inside), forward_cot, i - lead)
        when(i == nc - 1, cot_ready)
        both(-1, mm_pre, mm_back)
        both(LAG, act_hidden, act_grad)
        when(i == nc - 1 + LAG, peak_one)
        both(2 * LAG, hidden_out.forward, grad_out.forward)
        when(i + 2 < nc, cast_gate_up, i + 2)
        when((i + 2 >= nc) & (i + 2 < 2 * nc), cast_down, i + 2 - nc)
        when(i == nc + 1 + LAG, peak_two)
        for low, count, h in parts:
            at = first_in + low
            c = i - at + (0 if h is None else head)
            steps = count if h is None else count - 1
            if steps:
                when((i >= at) & (i < at + steps), in_step, c, h)
        when(i == first_in + nc - 1, in_last, 0)
        when(i == first_in, peak_three)
        when(i == first_in + 1, out_all)
        when(i == min(lead, nc - 1), turn_tokens)
        for n, k in enumerate(y_mid):
            when(i == first_in + 4 + n, y_pass, 0, k)

    first_in = nc + 2 * LAG + 1
    cast_gate_up(0)
    g_finish(0)
    for b in range(nb):
        cols = slice(b * band, (b + 1) * band)
        raw = all_tok[:, :, :, cols].reshape(total_t, band)
        r["tok"][:, cols] = soft(dot(raw, r["tab_w"][...]) * tok_inv)
    mm_pre(0, None)
    (cast_gate_up(1) if nc > 1 else cast_down(0))
    loop(0, max(first_in + nc + tail - 1, first_in + 4 + len(y_mid)), pipe)
    in_last(1)

    top2 = r["mid"][...]
    out_scale = lane_scalar(top2 * lane_scalar(top, 3) / (fp_top * fp_top), 0)

    def run_jobs(some):
        for body in (down_grads, gate_up_grads):
            at = [c for b, c in some if b is body]
            if at:
                body(at[0], at[-1] + 1)

    def gate_up_chunk(c):
        for b in range(nb):
            rows = slice(b * band, (b + 1) * band)
            for i, weight in enumerate((wg, wu)):
                weight[c, rows, :] = (
                    dot(r["tok_t"][rows, :], grad_out.rows(c, i)) * tok_unit
                ).astype(BF16)

    def gate_up_grads(low, high):
        loop(low, high, gate_up_chunk)

    passes = [(1 + h, k) for h in range(2) for k in y_mid]
    jobs = [(down_grads, c) for c in range(nc)] + [(gate_up_grads, c) for c in range(nc)]
    ahead, after = len(jobs) * 2 // 7, len(jobs) // 5
    between = len(jobs) - ahead - after
    done = 0
    for n, (i, k) in enumerate(passes):
        due = ahead + between * n // (len(passes) - 1)
        run_jobs(jobs[done:due])
        done = due
        y_pass(i, k)
    run_jobs(jobs[done:])
    r["output"][...] = (y_close(0).reshape(tl, wide) * out_scale).astype(BF16)
    pre.drain()
    back.drain()
    hidden_out.drain()
    grad_out.drain()
    for i in range(2):
        g_drain(i)
    for i in range(3):
        y_drain(i)
    for p in range(2):
        total = y_close(1 + p)
        for b in range(nb):
            cols = slice(b * band, (b + 1) * band)
            turned = dot_wide(total[:, cols], r["tab_w"][...]) * tok_s
            r["input_grad"][pl.ds(p * hl, hl), cols] = turned.astype(BF16)


def store_kernel(nc, piece, *refs):
    small, grads, outs, sems = refs[:2], refs[2:5], refs[5:10], refs[10]
    copies = [
        pltpu.make_async_copy(small[i], outs[i], sems.at[i, 0]) for i in range(2)
    ]
    for c in range(nc):
        cols = pl.ds(c * piece, piece)
        for i in range(3):
            dst = outs[2 + i].at[cols, :] if i == 2 else outs[2 + i].at[:, cols]
            copies.append(pltpu.make_async_copy(grads[i].at[c], dst, sems.at[2 + i, c]))
    for copy in copies:
        copy.start()
    for copy in copies:
        copy.wait()


def shards(nx, ny, tokens, cotangent, gate_weight, up_weight, down_weight):
    lanes = 1 << max((ny.bit_length() - 2) // 2, 0)
    tl, wide = tokens.shape
    hid = gate_weight.shape[1]
    piece = 256 if hid % 256 == 0 else hid
    band = 256 if wide % 256 == 0 else wide
    nc = hid // piece
    total_t = tl * ny
    hl, th = tl // 2, total_t // nx // 2
    tail = min(SPLIT, nc)
    x_outer, y_outer = nx // CORES, ny // lanes
    dims = (nx, ny, lanes, tl, wide, hid, piece, band)
    ins = ["tokens", "cot", "gate", "up", "down"]
    outs = ["output", "input_grad", "wg", "wu", "wd"]
    scratch = {
        "load": DMA((3, nc)), "own": DMA((2, 2)),
        "all_tok": pltpu.VMEM((2, ny, hl, wide), BF16),
        "all_cot": pltpu.VMEM((2, ny, hl, wide), BF16),
        "g_sf": DMA((2, 2)), "g_rf": DMA((2, y_outer)),
        "g_sn": DMA((2, 2)), "g_rn": DMA((2, 2)),
        "tab_w": pltpu.VMEM((band, band), BF16),
        "tab_h": pltpu.VMEM((piece, piece), BF16),
        "mid": pltpu.VMEM((1, 128), F32),
        "slots_x": pltpu.VMEM((nx, 1, 128), F32),
        "slots_y": pltpu.VMEM((ny, 1, 128), F32),
        "slots_x2": pltpu.VMEM((nx, 1, 128), F32),
        "slots_y2": pltpu.VMEM((ny, 1, 128), F32),
        "p_x": DMA((2,)), "p_y": DMA((2,)), "q_x": DMA((2,)), "q_y": DMA((2,)),
        "tok": pltpu.VMEM((total_t, wide), BF16),
        "tok_t": pltpu.VMEM((wide, total_t), BF16),
        "slope": pltpu.VMEM((nc, 2, 2, th, piece), F32),
        "hid": pltpu.VMEM((nc, total_t, piece), BF16),
        "acc": pltpu.VMEM((2, total_t // 2, wide), F32),
        "top_h": pltpu.VMEM((8, piece), F32),
        "out_part": pltpu.VMEM((2, ny, hl, wide), BF16),
        "in_part": pltpu.VMEM((2, ny, hl, wide), BF16),
        "y_one_o": pltpu.VMEM((y_outer, lanes - 1, 2, hl, wide), BF16),
        "y_two_o": pltpu.VMEM((y_outer - 1, 2, hl, wide), BF16),
        "y_three_o": pltpu.VMEM((y_outer - 1, 2, hl, wide), BF16),
        "y_one_i": pltpu.VMEM((2, y_outer, lanes - 1, hl, wide), BF16),
        "y_two_i": pltpu.VMEM((2, y_outer - 1, hl, wide), BF16),
        "y_three_i": pltpu.VMEM((2, y_outer - 1, hl, wide), BF16),
        "y_s1": DMA((3,)), "y_r1": DMA((3, y_outer)),
        "y_s2": DMA((3,)), "y_r2": DMA((3,)),
    }
    for tag, count, items in (("pre", 2, nc), ("back", 1, nc + tail)):
        block = (2, count, th, piece)
        scratch[tag + "_part"] = pltpu.VMEM((nc, 2, nx, count, th, piece), F32)
        scratch[tag + "_first"] = pltpu.VMEM((nc, x_outer, CORES - 1) + block, F32)
        scratch[tag + "_second"] = pltpu.VMEM((nc, x_outer - 1) + block, BF16)
        scratch[tag + "_third"] = pltpu.VMEM((nc, x_outer - 1) + block, BF16)
        scratch[tag + "_s"] = DMA((2,))
        scratch[tag + "_r1"] = DMA((items,))
        scratch[tag + "_r2"] = DMA((items, x_outer - 1))
    for tag, count, items in (("act_h", 1, nc), ("act_g", 2, nc + tail)):
        scratch[tag] = pltpu.VMEM((nc, 2, nx, count, th, piece), BF16)
        scratch[tag + "_s"] = DMA((2,))
        scratch[tag + "_rf"] = DMA((items, x_outer - 1))
        scratch[tag + "_rn"] = DMA((items,))
    names = tuple(ins + outs + list(scratch))
    small = jax.ShapeDtypeStruct(tokens.shape, BF16)
    small_vmem = pltpu.VMEM(tokens.shape, BF16)
    columns = pltpu.VMEM((nc, wide, piece), BF16)
    rows = pltpu.VMEM((nc, piece, wide), BF16)
    results = pl.pallas_call(
        functools.partial(layer_kernel, dims, names),
        out_shape=[small_vmem, small_vmem, columns, columns, rows],
        in_specs=[HBM] * 5,
        out_specs=[VMEM] * 5,
        scratch_shapes=list(scratch.values()),
        compiler_params=pltpu.CompilerParams(
            collective_id=0, has_side_effects=True, vmem_limit_bytes=VMEM_MIB * 2 ** 20
        ),
    )(tokens, cotangent, gate_weight, up_weight, down_weight)
    return pl.pallas_call(
        functools.partial(store_kernel, nc, piece),
        out_shape=[small, small] + [
            jax.ShapeDtypeStruct(w.shape, BF16)
            for w in (gate_weight, up_weight, down_weight)
        ],
        in_specs=[VMEM] * 5,
        out_specs=[HBM] * 5,
        scratch_shapes=[DMA((5, nc))],
        compiler_params=pltpu.CompilerParams(vmem_limit_bytes=STORE_MIB * 2 ** 20),
    )(*results)


def solution(mesh):
    in_specs = (P("gy", "gx"), P("gy", "gx"), P("gx", "gy"), P("gx", "gy"), P("gy", "gx"))
    out_specs = (P("gy", "gx"), P("gy", "gx"), P("gx", "gy"), P("gx", "gy"), P("gy", "gx"))
    nx, ny = mesh.shape["gx"], mesh.shape["gy"]
    return jax.shard_map(
        functools.partial(shards, nx, ny),
        mesh=mesh, in_specs=in_specs, out_specs=out_specs, check_vma=False,
    )
```

time: 73.6 us -> 73 us (level)
  no operation moved by 1% of the time
where the time goes in v3:
time: 73 us; the launch traced here: 72.9 us
  Pallas kernels  72.2 us (99%)
    pallas_call x1, Pallas kernels, shards(): pl.pallas_call(functools.partial(layer_kernel, dims, names), out_shape=[s...  67.8 us
    pallas_call x1, Pallas kernels, shards(): pl.pallas_call(functools.partial(store_kernel, nc, piece), out_shape=[sma...  4.42 us

profile of v3, /device:TPU:0, one launch (start us, length us, event | category | flops | bytes accessed | tf_op | source)
XLA Modules:
  0.0 72.9 jit_solution(17679572216753612255)
XLA Ops:
  0.6 67.8 %shard_map.92 = (bf16[32,1024]{1,0:T(8,128)(2,1)S(1)}, bf16[32,1024]{1,0:T(8,128)(2,1)S(1)}, bf16[7,1024,256]{2,1,0:T(8,128)(2,1)S(1)}, bf16[7,1024,256]{2,1,0:T(8,128)(2,1)S(1)}, bf16[7,256,1024]{2,1,0:T(8,128)(2,1)S(1)}) custom-call(bf16[32,1024]{1,0:T(8,128)(2,1)} %refs_0_.1, bf16[32,1024]{1,0:T(8,128)(2,1)} %refs_1_.1, bf16[1024,1792]{1,0:T(8,128)(2,1)} %refs_2_.1, ...), custom_call_target="tpu_custom_call" | custom-call | tf_op jit(solution)/shard_map/pallas_call | solution.py:772
  68.4 4.4 %shard_map.93 = (bf16[32,1024]{1,0:T(8,128)(2,1)}, bf16[32,1024]{1,0:T(8,128)(2,1)}, bf16[1024,1792]{1,0:T(8,128)(2,1)}, bf16[1024,1792]{1,0:T(8,128)(2,1)}, bf16[1792,1024]{1,0:T(8,128)(2,1)}) custom-call(bf16[32,1024]{1,0:T(8,128)(2,1)S(1)} %get-tuple-element.10.refs_0_, bf16[32,1024]{1,0:T(8,128)(2,1)S(1)} %get-tuple-element.11.refs_1_, ...), custom_call_target="tpu_custom_call" | custom-call | tf_op jit(solution)/shard_map/pallas_call | solution.py:782

commit v4 on v3

--- a/solution.py
+++ b/solution.py
@@ -194,7 +194,7 @@
     y_hi, y_lo = gy // lanes, lax.rem(gy, lanes)
     g_all = [all_tok, all_cot]
 
-    relay = wide // 4
+    relay = 3 * wide // 8 // 128 * 128
     cuts = pl.ds(0, wide - relay), pl.ds(wide - relay, relay)
 
     def g_far(i, p, k, slot):
@@ -514,8 +514,8 @@
             r["y_r2"].at[i], {"gy": lanes * j + y_lo},
         )
 
-    def y_send(i):
-        for k in y_order:
+    def y_send(i, order):
+        for k in order:
             for o in range(1, lanes):
                 y_near(i, k, o).start()
 
@@ -547,7 +547,7 @@
 
     def out_all():
         loop(0, nb, out_step)
-        y_send(0)
+        y_send(0, y_order)
 
     def y_drain(i):
         take(ones[i], r["y_s1"].at[i])
@@ -570,7 +570,7 @@
             rows = slice(b * band, (b + 1) * band)
             total = r["acc"][span(h), :, rows] + in_sum(nc - 1, h, rows)
             r["in_part"][h, :, :, rows] = total.astype(BF16).reshape(ny, hl, band)
-        y_send(1 + h)
+        y_send(1 + h, y_mid)
 
     r["acc"][...] = jnp.zeros((2, total_t // 2, wide), F32)
 
@@ -640,6 +640,8 @@
     (cast_gate_up(1) if nc > 1 else cast_down(0))
     loop(0, max(first_in + nc + tail - 1, first_in + 4 + len(y_mid)), pipe)
     in_last(1)
+    y_send(1, [0])
+    y_send(2, [0])
 
     top2 = r["mid"][...]
     out_scale = lane_scalar(top2 * lane_scalar(top, 3) / (fp_top * fp_top), 0)
@@ -663,7 +665,7 @@
 
     passes = [(1 + h, k) for h in range(2) for k in y_mid]
     jobs = [(down_grads, c) for c in range(nc)] + [(gate_up_grads, c) for c in range(nc)]
-    ahead, after = len(jobs) * 2 // 7, len(jobs) // 5
+    ahead, after = len(jobs) * 3 // 14, len(jobs) * 2 // 7
     between = len(jobs) - ahead - after
     done = 0
     for n, (i, k) in enumerate(passes):

time: 73 us -> 71.1 us (0.974)
  Pallas kernels: 72.2 us -> 70.3 us
    pallas_call x1, Pallas kernels: 67.8 us -> 65.9 us  [shards(): pl.pallas_call(functools.partial(layer_kernel, dims, names), out_shape=[s...]
where the time goes in v4:
time: 71.1 us; the launch traced here: 71 us
  Pallas kernels  70.3 us (99%)
    pallas_call x1, Pallas kernels, shards(): pl.pallas_call(functools.partial(layer_kernel, dims, names), out_shape=[s...  65.9 us
    pallas_call x1, Pallas kernels, shards(): pl.pallas_call(functools.partial(store_kernel, nc, piece), out_shape=[sma...  4.42 us

profile of v4, /device:TPU:0, one launch (start us, length us, event | category | flops | bytes accessed | tf_op | source)
XLA Modules:
  0.0 71.0 jit_solution(1586493980748430581)
XLA Ops:
  0.6 65.9 %shard_map.92 = (bf16[32,1024]{1,0:T(8,128)(2,1)S(1)}, bf16[32,1024]{1,0:T(8,128)(2,1)S(1)}, bf16[7,1024,256]{2,1,0:T(8,128)(2,1)S(1)}, bf16[7,1024,256]{2,1,0:T(8,128)(2,1)S(1)}, bf16[7,256,1024]{2,1,0:T(8,128)(2,1)S(1)}) custom-call(bf16[32,1024]{1,0:T(8,128)(2,1)} %refs_0_.1, bf16[32,1024]{1,0:T(8,128)(2,1)} %refs_1_.1, bf16[1024,1792]{1,0:T(8,128)(2,1)} %refs_2_.1, ...), custom_call_target="tpu_custom_call" | custom-call | tf_op jit(solution)/shard_map/pallas_call | solution.py:774
  66.6 4.4 %shard_map.93 = (bf16[32,1024]{1,0:T(8,128)(2,1)}, bf16[32,1024]{1,0:T(8,128)(2,1)}, bf16[1024,1792]{1,0:T(8,128)(2,1)}, bf16[1024,1792]{1,0:T(8,128)(2,1)}, bf16[1792,1024]{1,0:T(8,128)(2,1)}) custom-call(bf16[32,1024]{1,0:T(8,128)(2,1)S(1)} %get-tuple-element.10.refs_0_, bf16[32,1024]{1,0:T(8,128)(2,1)S(1)} %get-tuple-element.11.refs_1_, ...), custom_call_target="tpu_custom_call" | custom-call | tf_op jit(solution)/shard_map/pallas_call | solution.py:784
